TPU v7x, 32 devices: a whole 2x2x4 slice. The times are simulated.
32 devices in a mesh: gz: 2 (over core), row: 4 (over y, x), col: 4 (over z).
Axes of the slice: x: 2, y: 2, z: 4, core: 2. Of those that a mesh axis runs over, the one named last changes fastest.
Arguments:
- rhs_sub: float32 [2, 3, 4, 96, 256], P('gz', None, 'row', 'col'), may hold values from -6 to 6
- rhs_top: float32 [2, 4, 96, 256], P(None, 'row', 'col'), may hold values from -6 to 6
- lower_sub: bfloat16 [2, 3, 4, 4, 256, 256], P('gz', None, 'row', 'col'), may hold values from -0.078125 to 0.078125
- lower_link: bfloat16 [2, 2, 4, 4, 256, 256], P('gz', None, 'row', 'col'), may hold values from -0.078125 to 0.078125
- lower_top: bfloat16 [1, 4, 4, 256, 256], P(None, 'row', 'col'), may hold values from -0.078125 to 0.078125
- inv_sub: bfloat16 [2, 3, 4, 256, 256], P('gz', None, 'row'), may hold values from -0.3 to 1.3
- inv_top: bfloat16 [2, 4, 256, 256], P(None, 'row'), may hold values from -0.3 to 1.3
- mask_sub: int32 [2, 3, 4, 4], P('gz', None, 'row', 'col'), may hold values 0 or 1
- mask_link: int32 [2, 2, 4, 4], P('gz', None, 'row', 'col'), may hold values 0 or 1
- mask_top: int32 [1, 4, 4], P(None, 'row', 'col'), may hold values 0 or 1
Outputs:
- sol_sub: float32 [2, 3, 4, 96, 256], P('gz', None, 'row', 'col')
- sol_top: float32 [2, 4, 96, 256], P(None, 'row', 'col')
All inputs are finite; a program needn't handle non-finite values. No bound on the sum of `mask_sub` or of `mask_link` or of `mask_top` on one device may be relied on, other than what follows from the above.
Results may differ from a plain program's by a relative error of at most 0.02.
Values may be sent and summed in bfloat16 or wider, within the bound.
No kernel may reach another device: no remote copies, remote signals or barrier semaphores. Data moves between devices by JAX's collectives and lax.ppermute only.
A program may use at most 64 MiB of HBM per device.

v0:
```python
import jax
import jax.numpy as jnp
from jax import lax
from jax.sharding import PartitionSpec as P


def forward_terms(column_vectors, blocks, pattern):
    product = jnp.einsum(
        "jnb,ijbd->ijnd", column_vectors, blocks, preferred_element_type=jnp.float32
    )
    return jnp.sum(product * pattern.astype(jnp.float32)[:, :, None, None], axis=1)


def backward_terms(row_vectors, blocks, pattern):
    product = jnp.einsum("knd,kjbd->kjnb", row_vectors, blocks, preferred_element_type=jnp.float32)
    return jnp.sum(product * pattern.astype(jnp.float32)[:, :, None, None], axis=0)


def inverse_rows(residual, inverse):
    return jnp.einsum(
        "inb,ibd->ind", residual.astype(jnp.bfloat16), inverse, preferred_element_type=jnp.float32
    )


def inverse_cols(residual, inverse):
    return jnp.einsum(
        "ind,ibd->inb", residual.astype(jnp.bfloat16), inverse, preferred_element_type=jnp.float32
    )


def own_share(values, share_cols):
    return lax.dynamic_slice_in_dim(values, lax.axis_index("col") * share_cols, share_cols, 1)


def level_solve(partial_sum, rhs_local, inverse, gate_value, across_groups):
    share_cols = rhs_local.shape[1]
    col_index = lax.axis_index("col")
    placed = lax.dynamic_update_slice_in_dim(
        jnp.zeros_like(partial_sum), rhs_local * gate_value, col_index * share_cols, 1
    )
    residual = lax.psum((placed - partial_sum).astype(jnp.bfloat16), "col").astype(jnp.float32)
    if across_groups:
        residual = lax.psum(residual.astype(jnp.bfloat16), "gz").astype(jnp.float32)
    result = inverse_rows(residual, inverse)
    return result


def column_vectors(rounded, col_blocks):
    col_index = lax.axis_index("col")
    every_block = lax.all_gather(rounded, "row", axis=0, tiled=True)
    result = lax.dynamic_slice_in_dim(every_block, col_index * col_blocks, col_blocks, 0)
    return result


def back_solve(back_part, solved_rows, inverse, share_cols):
    row_blocks = solved_rows.shape[0]
    summed = lax.psum(back_part.astype(jnp.bfloat16), "row").astype(jnp.float32)
    every_block = lax.all_gather(summed.astype(jnp.bfloat16), "col", axis=0, tiled=True).astype(
        summed.dtype
    )
    own_rows = lax.dynamic_slice_in_dim(
        every_block, lax.axis_index("row") * row_blocks, row_blocks, 0
    )
    answer = inverse_cols(solved_rows - own_rows, inverse)
    share = own_share(answer, share_cols)
    half = answer.astype(jnp.bfloat16)
    return (share, half)


def per_device(
    rhs_sub,
    rhs_top,
    lower_sub,
    lower_link,
    lower_top,
    inv_sub,
    inv_top,
    mask_sub,
    mask_link,
    mask_top,
):
    sub_levels = inv_sub.shape[1]
    top_levels = inv_top.shape[0]
    col_blocks = lower_top.shape[2]
    share_cols = rhs_top.shape[2]
    group_gate = (lax.axis_index("gz") == 0).astype(jnp.float32)
    unit_gate = jnp.float32(1.0)
    row_shape = (inv_top.shape[1], share_cols * lax.axis_size("col"), inv_top.shape[-1])
    column_shape = (col_blocks, row_shape[1], row_shape[2])
    sub_solved = []
    sub_columns = []
    for tier_index in range(sub_levels):
        partial_sum = jnp.zeros(row_shape, jnp.float32)
        for earlier in range(tier_index):
            pair_index = tier_index * (tier_index - 1) // 2 + earlier
            partial_sum = partial_sum + forward_terms(
                sub_columns[earlier], lower_sub[0, pair_index], mask_sub[0, pair_index]
            )
        solved = level_solve(
            partial_sum, rhs_sub[0, tier_index], inv_sub[0, tier_index], unit_gate, False
        )
        sub_solved.append(solved)
        sub_columns.append(column_vectors(solved.astype(jnp.bfloat16), col_blocks))
    top_solved = []
    top_columns = []
    for top_level in range(top_levels):
        partial_sum = forward_terms(
            sub_columns[sub_levels - 1], lower_link[0, top_level], mask_link[0, top_level]
        )
        for earlier in range(top_level):
            pair_index = top_level * (top_level - 1) // 2 + earlier
            partial_sum = partial_sum + group_gate * forward_terms(
                top_columns[earlier], lower_top[pair_index], mask_top[pair_index]
            )
        solved = level_solve(partial_sum, rhs_top[top_level], inv_top[top_level], group_gate, True)
        top_solved.append(solved)
        if top_level + 1 < top_levels:
            top_columns.append(column_vectors(solved.astype(jnp.bfloat16), col_blocks))
    top_share = [None] * top_levels
    top_half = [None] * top_levels
    for top_level in reversed(range(top_levels)):
        if top_level + 1 == top_levels:
            answer = inverse_cols(top_solved[top_level], inv_top[top_level])
            share = own_share(answer, share_cols)
            half = answer.astype(jnp.bfloat16)
        else:
            later_level = 1
            pair_index = later_level * (later_level - 1) // 2 + top_level
            back_part = backward_terms(
                top_half[later_level], lower_top[pair_index], mask_top[pair_index]
            )
            share, half = back_solve(
                back_part, top_solved[top_level], inv_top[top_level], share_cols
            )
        top_share[top_level] = share
        top_half[top_level] = half
    sub_share = [None] * sub_levels
    sub_half = [None] * sub_levels
    for tier_index in reversed(range(sub_levels)):
        back_part = jnp.zeros(column_shape, jnp.float32)
        for later_level in range(tier_index + 1, sub_levels):
            pair_index = later_level * (later_level - 1) // 2 + tier_index
            back_part = back_part + backward_terms(
                sub_half[later_level], lower_sub[0, pair_index], mask_sub[0, pair_index]
            )
        if tier_index == sub_levels - 1:
            for top_level in range(top_levels):
                back_part = back_part + backward_terms(
                    top_half[top_level], lower_link[0, top_level], mask_link[0, top_level]
                )
        share, half = back_solve(
            back_part, sub_solved[tier_index], inv_sub[0, tier_index], share_cols
        )
        sub_share[tier_index] = share
        sub_half[tier_index] = half
    sol_sub = jnp.stack(sub_share)[None]
    sol_top = jnp.stack(top_share)
    return (sol_sub, sol_top)


def solution(mesh):
    return jax.shard_map(
        per_device,
        mesh=mesh,
        in_specs=(
            P("gz", None, "row", "col", None),
            P(None, "row", "col", None),
            P("gz", None, "row", "col", None, None),
            P("gz", None, "row", "col", None, None),
            P(None, "row", "col", None, None),
            P("gz", None, "row", None, None),
            P(None, "row", None, None),
            P("gz", None, "row", "col"),
            P("gz", None, "row", "col"),
            P(None, "row", "col"),
        ),
        out_specs=(P("gz", None, "row", "col", None), P(None, "row", "col", None)),
        check_vma=False,
    )
```

profile of v0, /device:TPU:6, one launch (start us, length us, event | category | flops | bytes accessed | tf_op | source)
XLA Modules:
  0.0 259.2 jit_solution(2911516491720442301)
XLA Ops:
  0.7 0.8 bitcast_dynamic-update-slice_fusion.4
  1.5 19.8 %psum.77 = bf16[96,256]{1,0:T(8,128)(2,1)S(1)} all-reduce(bf16[96,256]{1,0:T(8,128)(2,1)S(1)} %convert_bitcast_fusion), channel_id=1, replica_groups=mesh['gz'=2,'row'=4,'col'=4] {'col'}, use_global_device_ids=true, to_apply=%region_0.0 | all-reduce | flops 24576 | bytes 98304 | tf_op jit(solution)/shard_map/psum | solution.py:41
  21.3 0.2 fusion.124
  21.5 7.7 %all-gather = bf16[384,256]{1,0:T(8,128)(2,1)S(1)} all-gather(bf16[96,256]{1,0:T(8,128)(2,1)S(1)} %get-tuple-element.7), channel_id=2, replica_groups=mesh['gz'=2,'row'=4,'col'=4] {'row'}, dimensions={0}, use_global_device_ids=true | all-gather | bytes 245760 | tf_op jit(solution)/shard_map/all_gather | solution.py:50
  29.2 0.9 copy-done.5
  30.1 0.6 copy-done.7
  30.8 0.6 fusion.123
  32.0 0.2 fusion.26
  32.2 16.1 %psum.78 = bf16[96,256]{1,0:T(8,128)(2,1)S(1)} all-reduce(bf16[96,256]{1,0:T(8,128)(2,1)S(1)} %fusion.26), channel_id=1, replica_groups=mesh['gz'=2,'row'=4,'col'=4] {'col'}, use_global_device_ids=true, to_apply=%region_1.0 | all-reduce | flops 24576 | bytes 98304 | tf_op jit(solution)/shard_map/psum | solution.py:41
  48.3 0.2 fusion.125
  48.4 8.7 %all-gather.1 = bf16[384,256]{1,0:T(8,128)(2,1)S(1)} all-gather(bf16[96,256]{1,0:T(8,128)(2,1)S(1)} %get-tuple-element.9), channel_id=3, replica_groups=mesh['gz'=2,'row'=4,'col'=4] {'row'}, dimensions={0}, use_global_device_ids=true | all-gather | bytes 245760 | tf_op jit(solution)/shard_map/all_gather | solution.py:50
  57.7 0.2 convolution_multiply_fusion.9
  58.6 0.2 fusion.27
  58.7 18.0 %psum.79 = bf16[96,256]{1,0:T(8,128)(2,1)S(1)} all-reduce(bf16[96,256]{1,0:T(8,128)(2,1)S(1)} %fusion.27), channel_id=1, replica_groups=mesh['gz'=2,'row'=4,'col'=4] {'col'}, use_global_device_ids=true, to_apply=%region_2.0 | all-reduce | flops 24576 | bytes 98304 | tf_op jit(solution)/shard_map/psum | solution.py:41
  76.7 0.2 fusion.126
  76.9 7.9 %all-gather.2 = bf16[384,256]{1,0:T(8,128)(2,1)S(1)} all-gather(bf16[96,256]{1,0:T(8,128)(2,1)S(1)} %get-tuple-element.11), channel_id=4, replica_groups=mesh['gz'=2,'row'=4,'col'=4] {'row'}, dimensions={0}, use_global_device_ids=true | all-gather | bytes 245760 | tf_op jit(solution)/shard_map/all_gather | solution.py:50
  84.8 0.8 copy-done.6
  85.6 0.6 copy-done.8
  86.2 0.6 fusion.122
  87.5 0.2 fusion.17
  87.7 16.1 %psum.80 = bf16[1,96,256]{2,1,0:T(8,128)(2,1)S(1)} all-reduce(bf16[1,96,256]{2,1,0:T(8,128)(2,1)S(1)} %fusion.17), channel_id=1, replica_groups=mesh['gz'=2,'row'=4,'col'=4] {'col'}, use_global_device_ids=true, to_apply=%region_3.0 | all-reduce | flops 24576 | bytes 98304 | tf_op jit(solution)/shard_map/psum | solution.py:41
  103.8 3.5 %psum.81 = bf16[96,256]{1,0:T(8,128)(2,1)S(1)} all-reduce(bf16[96,256]{1,0:T(8,128)(2,1)S(1)} %bitcast.253), channel_id=1, replica_groups=mesh['gz'=2,'row'=4,'col'=4] {'gz'}, use_global_device_ids=true, to_apply=%region_4.0 | all-reduce | flops 24576 | bytes 98304 | tf_op jit(solution)/shard_map/psum | solution.py:43
  107.5 8.7 %all-gather.3 = bf16[384,256]{1,0:T(8,128)(2,1)S(1)} all-gather(bf16[96,256]{1,0:T(8,128)(2,1)S(1)} %get-tuple-element.13), channel_id=5, replica_groups=mesh['gz'=2,'row'=4,'col'=4] {'row'}, dimensions={0}, use_global_device_ids=true | all-gather | bytes 245760 | tf_op jit(solution)/shard_map/all_gather | solution.py:50
  116.9 0.2 fusion.6
  117.8 0.2 fusion.16
  117.9 18.0 %psum.82 = bf16[1,96,256]{2,1,0:T(8,128)(2,1)S(1)} all-reduce(bf16[1,96,256]{2,1,0:T(8,128)(2,1)S(1)} %fusion.16), channel_id=1, replica_groups=mesh['gz'=2,'row'=4,'col'=4] {'col'}, use_global_device_ids=true, to_apply=%region_5.0 | all-reduce | flops 24576 | bytes 98304 | tf_op jit(solution)/shard_map/psum | solution.py:41
  136.0 3.5 %psum.83 = bf16[96,256]{1,0:T(8,128)(2,1)S(1)} all-reduce(bf16[96,256]{1,0:T(8,128)(2,1)S(1)} %bitcast.254), channel_id=1, replica_groups=mesh['gz'=2,'row'=4,'col'=4] {'gz'}, use_global_device_ids=true, to_apply=%region_6.0 | all-reduce | flops 24576 | bytes 98304 | tf_op jit(solution)/shard_map/psum | solution.py:43
  139.5 0.3 fusion.21
  139.8 0.2 fusion.23
  140.0 14.8 %psum.84 = bf16[1,96,256]{2,1,0:T(8,128)(2,1)S(1)} all-reduce(bf16[1,96,256]{2,1,0:T(8,128)(2,1)S(1)} %fusion.23), channel_id=1, replica_groups=mesh['gz'=2,'row'=4,'col'=4] {'row'}, use_global_device_ids=true, to_apply=%region_7.0 | all-reduce | flops 24576 | bytes 98304 | tf_op jit(solution)/shard_map/psum | solution.py:57
  154.8 13.7 %all_gather.28 = bf16[4,96,256]{2,1,0:T(8,128)(2,1)S(1)} all-gather(bf16[1,96,256]{2,1,0:T(8,128)(2,1)S(1)} %psum.84), channel_id=1, replica_groups=mesh['gz'=2,'row'=4,'col'=4] {'col'}, dimensions={0}, use_global_device_ids=true | all-gather | bytes 245760 | tf_op jit(solution)/shard_map/all_gather | solution.py:58
  168.5 0.2 fusion.34
  168.7 0.6 pad_maximum_fusion
  169.4 0.2 convolution_multiply_fusion.3
  169.6 0.2 fusion.24
  169.8 15.7 %psum.85 = bf16[1,96,256]{2,1,0:T(8,128)(2,1)S(1)} all-reduce(bf16[1,96,256]{2,1,0:T(8,128)(2,1)S(1)} %fusion.24), channel_id=1, replica_groups=mesh['gz'=2,'row'=4,'col'=4] {'row'}, use_global_device_ids=true, to_apply=%region_8.0 | all-reduce | flops 24576 | bytes 98304 | tf_op jit(solution)/shard_map/psum | solution.py:57
  185.5 13.6 %all_gather.29 = bf16[4,96,256]{2,1,0:T(8,128)(2,1)S(1)} all-gather(bf16[1,96,256]{2,1,0:T(8,128)(2,1)S(1)} %psum.85), channel_id=1, replica_groups=mesh['gz'=2,'row'=4,'col'=4] {'col'}, dimensions={0}, use_global_device_ids=true | all-gather | bytes 245760 | tf_op jit(solution)/shard_map/all_gather | solution.py:58
  199.0 0.2 fusion.40
  199.2 0.2 fusion.22
  199.4 15.3 %psum.86 = bf16[1,96,256]{2,1,0:T(8,128)(2,1)S(1)} all-reduce(bf16[1,96,256]{2,1,0:T(8,128)(2,1)S(1)} %fusion.22), channel_id=1, replica_groups=mesh['gz'=2,'row'=4,'col'=4] {'row'}, use_global_device_ids=true, to_apply=%region_9.0 | all-reduce | flops 24576 | bytes 98304 | tf_op jit(solution)/shard_map/psum | solution.py:57
  214.7 13.7 %all_gather.30 = bf16[4,96,256]{2,1,0:T(8,128)(2,1)S(1)} all-gather(bf16[1,96,256]{2,1,0:T(8,128)(2,1)S(1)} %psum.86), channel_id=1, replica_groups=mesh['gz'=2,'row'=4,'col'=4] {'col'}, dimensions={0}, use_global_device_ids=true | all-gather | bytes 245760 | tf_op jit(solution)/shard_map/all_gather | solution.py:58
  228.4 0.2 fusion.48
  228.6 0.2 convolution_multiply_fusion
  228.8 0.2 fusion.25
  229.0 15.7 %psum.87 = bf16[1,96,256]{2,1,0:T(8,128)(2,1)S(1)} all-reduce(bf16[1,96,256]{2,1,0:T(8,128)(2,1)S(1)} %fusion.25), channel_id=1, replica_groups=mesh['gz'=2,'row'=4,'col'=4] {'row'}, use_global_device_ids=true, to_apply=%region_10.0 | all-reduce | flops 24576 | bytes 98304 | tf_op jit(solution)/shard_map/psum | solution.py:57
  244.7 13.6 %all_gather.31 = bf16[4,96,256]{2,1,0:T(8,128)(2,1)S(1)} all-gather(bf16[1,96,256]{2,1,0:T(8,128)(2,1)S(1)} %psum.87), channel_id=1, replica_groups=mesh['gz'=2,'row'=4,'col'=4] {'col'}, dimensions={0}, use_global_device_ids=true | all-gather | bytes 245760 | tf_op jit(solution)/shard_map/all_gather | solution.py:58
  258.3 0.2 fusion.54
  258.5 0.6 maximum_bitcast_fusion
  (30 shorter events, 0.4 us)
Async XLA Ops:
  0.6 116.3 %copy-start = (bf16[1,1,1,256,256]{4,3,2,1,0:T(8,128)(2,1)S(1)}, bf16[1,1,1,256,256]{4,3,2,1,0:T(8,128)(2,1)}, u32[]{:S(2)}) copy-start(bf16[1,1,1,256,256]{4,3,2,1,0:T(8,128)(2,1)} %param.14) | copy-start | bytes 393220
  0.6 20.6 %copy-start.2 = (bf16[1,3,1,256,256]{4,3,2,1,0:T(8,128)(2,1)S(1)}, bf16[1,3,1,256,256]{4,3,2,1,0:T(8,128)(2,1)}, u32[]{:S(2)}) copy-start(bf16[1,3,1,256,256]{4,3,2,1,0:T(8,128)(2,1)} %param.15) | copy-start | bytes 1179652
  21.3 10.7 %copy-start.1 = (bf16[1,3,1,1,256,256]{5,4,3,2,1,0:T(8,128)(2,1)S(1)}, bf16[1,3,1,1,256,256]{5,4,3,2,1,0:T(8,128)(2,1)}, u32[]{:S(2)}) copy-start(bf16[1,3,1,1,256,256]{5,4,3,2,1,0:T(8,128)(2,1)} %param.12) | copy-start | bytes 1179652
  29.2 0.9 copy-start.5
  30.1 0.7 copy-start.7
  76.9 10.6 %copy-start.3 = (bf16[1,2,1,1,256,256]{5,4,3,2,1,0:T(8,128)(2,1)S(1)}, bf16[1,2,1,1,256,256]{5,4,3,2,1,0:T(8,128)(2,1)}, u32[]{:S(2)}) copy-start(bf16[1,2,1,1,256,256]{5,4,3,2,1,0:T(8,128)(2,1)} %param.13) | copy-start | bytes 786436
  84.8 0.8 copy-start.6
  85.6 0.7 copy-start.8
  87.5 19.8 %copy-start.4 = (bf16[2,1,256,256]{3,2,1,0:T(8,128)(2,1)S(1)}, bf16[2,1,256,256]{3,2,1,0:T(8,128)(2,1)}, u32[]{:S(2)}) copy-start(bf16[2,1,256,256]{3,2,1,0:T(8,128)(2,1)} %param.16) | copy-start | bytes 786436
where the time goes:
time: 262 us; the launch traced here: 259 us
  blocking collectives  244 us (93%)
  local copies, waits for them, and re-layouts  5.17 us (2%)
  between operations  4.84 us (2%)
  matrix products  3.71 us (1%)
    psum x5, blocking collectives, level_solve(): lax.psum((placed - partial_sum).astype(jnp.bfloat16), 'col')  88 us
    psum x4, blocking collectives, back_solve(): summed = lax.psum(back_part.astype(jnp.bfloat16), 'row').astype(jnp.float32)  61.6 us
    all_gather x4, blocking collectives, back_solve(): lax.all_gather(summed.astype(jnp.bfloat16), 'col', axis=0, tiled=True)  54.5 us
    all_gather x4, blocking collectives, column_vectors(): every_block = lax.all_gather(rounded, 'row', axis=0, tiled=True)  33 us
    psum x2, blocking collectives, level_solve(): residual = lax.psum(residual.astype(jnp.bfloat16), 'gz').astype(jnp.float32)  7.06 us

commit v1 on v0

v1 whole, which is shorter than its diff:
```python
import jax
import jax.numpy as jnp
from jax import lax
from jax.sharding import PartitionSpec as P

BF = jnp.bfloat16
F32 = jnp.float32


def ring_from(values, axis, step):
    size = lax.axis_size(axis)
    if step == 0:
        return values
    return lax.ppermute(values, axis, [((d + step) % size, d) for d in range(size)])


def rolled(stack, start):
    size = stack.shape[0]
    return lax.dynamic_slice_in_dim(jnp.concatenate([stack, stack]), start % size, size, 0)


def row_gather(block):
    return [ring_from(block, "row", p) for p in range(lax.axis_size("row"))]


def scaled(lower, pattern, inverse):
    kept = lower * pattern.astype(BF)[:, :, None, None]
    return jnp.einsum("ijbd,ide->ijbe", kept, inverse, preferred_element_type=F32).astype(BF)


def spread(vectors, gathered):
    return jnp.stack(
        [jnp.einsum("jnb,ijbd->ind", vectors, g, preferred_element_type=F32) for g in gathered]
    )


def to_owners(parts, levels):
    rows, cols = lax.axis_size("row"), lax.axis_size("col")
    r, j = lax.axis_index("row"), lax.axis_index("col")
    parts = parts.astype(BF)
    if rows == cols:
        total = lax.dynamic_index_in_dim(parts, (j - r) % rows, 0, False).astype(F32)
        for s in range(1, cols):
            send = lax.dynamic_index_in_dim(parts, (j + s - r) % rows, 0, False)
            got = lax.ppermute(send, "col", [(d, (d + s) % cols) for d in range(cols)])
            total = total + got.astype(F32)
        return total
    natural = rolled(parts, rows - r)
    natural = jnp.moveaxis(natural, 1, 2)
    natural = natural.reshape((cols, -1) + natural.shape[2:])
    got = lax.all_to_all(natural, "col", 0, 0, tiled=True)
    return jnp.moveaxis(jnp.sum(got.astype(F32), axis=0), 1, 0)


def from_owners(vectors):
    rows, cols = lax.axis_size("row"), lax.axis_size("col")
    r, j = lax.axis_index("row"), lax.axis_index("col")
    if rows == cols:
        stack = jnp.stack([ring_from(vectors, "col", s) for s in range(cols)])
        return rolled(stack, r - j)
    stack = lax.all_gather(vectors, "col", axis=1, tiled=True)
    stack = stack.reshape((stack.shape[0], rows, -1) + stack.shape[2:])
    return rolled(jnp.moveaxis(stack, 1, 0), r)


def collect(rel, index, gathered):
    total = 0.0
    for p, g in enumerate(gathered):
        total = total + jnp.einsum("knd,kjbd->jnb", rel[p, index], g, preferred_element_type=F32)
    return total


def owner_pairs(rows, cols):
    wide = cols // rows
    return [
        (a * cols + c, (c % rows) * cols + a * wide + c // rows)
        for a in range(rows)
        for c in range(cols)
    ]


def into_owner_layout(values, col_blocks):
    rows, cols = lax.axis_size("row"), lax.axis_size("col")
    if rows != cols:
        c = lax.axis_index("col")
        values = lax.all_gather(values, "col", axis=2, tiled=True)
        n = values.shape[2] // rows
        values = lax.dynamic_slice_in_dim(values, (c // rows) * col_blocks, col_blocks, 1)
        values = lax.dynamic_slice_in_dim(values, (c % rows) * n, n, 2)
    return lax.ppermute(values, ("row", "col"), owner_pairs(rows, cols))


def from_owner_layout(values, share):
    rows, cols = lax.axis_size("row"), lax.axis_size("col")
    values = lax.ppermute(values, ("row", "col"), [(b, a) for a, b in owner_pairs(rows, cols)])
    if rows != cols:
        every = lax.all_gather(values, "col", axis=0)
        every = every.reshape((cols // rows, rows) + every.shape[1:])
        every = every.transpose(2, 0, 3, 1, 4, 5)
        every = every.reshape(
            every.shape[0], every.shape[1] * every.shape[2], -1, every.shape[5]
        )
        values = lax.dynamic_slice_in_dim(every, lax.axis_index("col") * share, share, 2)
    return values


def pair_of(later, earlier):
    return later * (later - 1) // 2 + earlier


def per_device(
    rhs_sub,
    rhs_top,
    lower_sub,
    lower_link,
    lower_top,
    inv_sub,
    inv_top,
    mask_sub,
    mask_link,
    mask_top,
):
    subs = inv_sub.shape[1]
    tops = inv_top.shape[0]
    col_blocks = lower_top.shape[2]
    share = rhs_top.shape[2]
    levels = subs + tops
    inverse = [inv_sub[0, l] for l in range(subs)] + [inv_top[t] for t in range(tops)]
    rhs = [rhs_sub[0, l] for l in range(subs)] + [rhs_top[t] for t in range(tops)]

    def factor(a, b):
        if a < subs:
            p = pair_of(a, b)
            return scaled(lower_sub[0, p], mask_sub[0, p], inverse[a])
        if b < subs:
            return scaled(lower_link[0, a - subs], mask_link[0, a - subs], inverse[a])
        p = pair_of(a - subs, b - subs)
        return scaled(lower_top[p], mask_top[p], inverse[a])

    scaled_rhs = jnp.stack(
        [
            jnp.einsum("ind,ide->ine", v.astype(BF), w, preferred_element_type=F32).astype(BF)
            for v, w in zip(rhs, inverse)
        ]
    )
    owned = into_owner_layout(scaled_rhs, col_blocks)
    base = [owned[l].astype(F32) for l in range(levels)]
    pairs = [(a, b) for a in range(levels) for b in range(a) if a < subs or b >= subs - 1]
    gathered = {ab: row_gather(factor(*ab)) for ab in pairs}

    solved = []
    for a in range(levels):
        value = base[a]
        near = [b for b in range(a) if (a, b) in gathered]
        own = [b for b in near if a < subs or b >= subs]
        cross = [b for b in near if b not in own]
        for group, across in ((own, False), (cross, True)):
            if group:
                parts = sum(spread(solved[b].astype(BF), gathered[a, b]) for b in group)
                total = to_owners(parts[:, None], 1)[0]
                if across:
                    both = lax.all_gather(total.astype(BF), "gz").astype(F32)
                    total = jnp.sum(both, axis=0)
                value = value - total
        solved.append(value)

    back = [None] * levels
    arrived = {}
    for b in reversed(range(levels)):
        value = solved[b]
        for a in range(b + 1, levels):
            if (a, b) in gathered:
                value = value - collect(arrived[a], 0, gathered[a, b])
        back[b] = value.astype(BF)
        if b:
            arrived[b] = from_owners(back[b][None])

    answers = []
    for l in range(levels):
        rows_back = from_owner_layout(back[l][None], share)[0]
        answers.append(
            jnp.einsum("ind,ibd->inb", rows_back, inverse[l], preferred_element_type=F32)
        )
    return jnp.stack(answers[:subs])[None], jnp.stack(answers[subs:])


def solution(mesh):
    return jax.shard_map(
        per_device,
        mesh=mesh,
        in_specs=(
            P("gz", None, "row", "col", None),
            P(None, "row", "col", None),
            P("gz", None, "row", "col", None, None),
            P("gz", None, "row", "col", None, None),
            P(None, "row", "col", None, None),
            P("gz", None, "row", None, None),
            P(None, "row", None, None),
            P("gz", None, "row", "col"),
            P("gz", None, "row", "col"),
            P(None, "row", "col"),
        ),
        out_specs=(P("gz", None, "row", "col", None), P(None, "row", "col", None)),
        check_vma=False,
    )
```

time: 262 us -> 131 us (0.50)
  blocking collectives: 244 us -> 3.65 us
  starting transfers between devices: 0 us -> 83.1 us
  waiting for transfers between devices: 0 us -> 21.8 us
  matrix products: 3.71 us -> 14.6 us
  local copies, waits for them, and re-layouts: 5.17 us -> 2.11 us
  between operations: 4.84 us -> 2.07 us
    psum x11 -> x0, blocking collectives: 157 us -> none  [the longest x5 88 us: level_solve(): lax.psum((placed - partial_sum).astype(jnp.bfloat16), 'col')]
    all_gather x8 -> x2, blocking collectives: 87.5 us -> 3.65 us  [per_device(): both = lax.all_gather(total.astype(BF), 'gz').astype(F32)]
    ppermute x0 -> x51, starting transfers between devices: none -> 83.1 us  [the longest x30 33.4 us: ring_from(): lax.ppermute(values, axis, [((d + step) % size, d) for d in range(size)])]
    ppermute x0 -> x51, waiting for transfers between devices: none -> 21.8 us  [the longest x30 13.5 us: ring_from(): lax.ppermute(values, axis, [((d + step) % size, d) for d in range(size)])]
    dot_general x21 -> x64, matrix products: 3.71 us -> 14.6 us  [the longest x6 5.34 us: scaled(): jnp.einsum('ijbd,ide->ijbe', kept, inverse, preferred_element_type=F32)]
  transfers between devices with their start and end apart: 0 -> 51, of which waited for: 0 -> 12; matrix products, arithmetic and copies ran while one was open for 0% -> 12% of each run, Pallas kernels for 0% -> 0%
where the time goes in v1:
time: 131 us; the launch traced here: 130 us
  starting transfers between devices  83.1 us (63%)
  waiting for transfers between devices  21.8 us (17%)
  matrix products  14.6 us (11%)
  blocking collectives  3.65 us (3%)
  other arithmetic  3.15 us (2%)
  local copies, waits for them, and re-layouts  2.11 us (2%)
  between operations  2.07 us (2%)
    ppermute x30, starting transfers between devices, ring_from(): lax.ppermute(values, axis, [((d + step) % size, d) for d in range(size)])  33.4 us
    ppermute x5, starting transfers between devices, from_owner_layout(): lax.ppermute(values, ('row', 'col'), [(b, a) for a, b in owner_pairs(rows...  25.3 us
    ppermute x15, starting transfers between devices, to_owners(): got = lax.ppermute(send, 'col', [(d, (d + s) % cols) for d in range(cols)])  18.9 us
    ppermute x30, waiting for transfers between devices, ring_from(): lax.ppermute(values, axis, [((d + step) % size, d) for d in range(size)])  13.5 us
    ppermute x1, starting transfers between devices, into_owner_layout(): return lax.ppermute(values, ('row', 'col'), owner_pairs(rows, cols))  5.55 us
    dot_general x6, matrix products, scaled(): jnp.einsum('ijbd,ide->ijbe', kept, inverse, preferred_element_type=F32)  5.34 us
    ppermute x5, waiting for transfers between devices, from_owner_layout(): lax.ppermute(values, ('row', 'col'), [(b, a) for a, b in owner_pairs(rows...  4.41 us
    dot_general x24, matrix products, collect(): jnp.einsum('knd,kjbd->jnb', rel[p, index], g, preferred_element_type=F32)  4.3 us
  transfers between devices with their start and end apart: 51, of which 12 were waited for; matrix products, arithmetic and copies ran while one was open for 12% of the time, Pallas kernels for 0%

profile of v1, /device:TPU:6, one launch (start us, length us, event | category | flops | bytes accessed | tf_op | source)
XLA Modules:
  0.0 130.5 jit_solution(7617572962592000045)
XLA Ops:
  0.6 0.7 convert.120
  2.0 1.8 %convolution_convert_fusion.5 = bf16[256,256]{1,0:T(8,128)(2,1)S(1)} fusion(bf16[1,3,1,1,256,256]{5,4,3,2,1,0:T(8,128)(2,1)} %param.12, bf16[1,3,1,256,256]{4,3,2,1,0:T(8,128)(2,1)} %param.15, bf16[]{:T(256)} %bitcast.16), kind=kOutput, calls=%fused_computation.5 | convolution fusion | flops 33685504 | bytes 393728 | tf_op jit(solution)/shard_map/ijbd,ide->ijbe/dot_general | solution.py:28
  4.5 2.8 %collective-permute-start.3 = (bf16[1,1,256,256]{3,2,1,0:T(8,128)(2,1)S(1)}, bf16[1,1,256,256]{3,2,1,0:T(8,128)(2,1)S(1)}, u32[]{:S(2)}, u32[]{:S(2)}) collective-permute-start(bf16[1,1,256,256]{3,2,1,0:T(8,128)(2,1)S(1)} %bitcast.655), channel_id=1, source_target_pairs={{12,0},{0,4},{4,8},{8,12},{13,1},{1,5},{5,9},{9,13},{14,2},{2,6},{... | collective-permute-start | bytes 393224 | tf_op jit(solution)/shard_map/ppermute | solution.py:14
  7.3 0.9 convert.118
  9.6 5.5 %collective-permute-start = (bf16[5,1,24,256]{3,2,1,0:T(8,128)(2,1)S(1)}, bf16[5,1,24,256]{3,2,1,0:T(8,128)(2,1)S(1)}, u32[]{:S(2)}, u32[]{:S(2)}) collective-permute-start(bf16[5,1,24,256]{3,2,1,0:T(8,128)(2,1)S(1)} %fusion.21), channel_id=1, source_target_pairs={{0,0},{1,4},{2,8},{3,12},{4,1},{5,5},{6,9},{7,13},{8,2},{9,6},{10,... | collective-permute-start | bytes 184328 | tf_op jit(solution)/shard_map/ppermute | solution.py:90
  15.2 0.9 convolution_convert_fusion.4
  16.1 0.8 convolution_convert_fusion.3
  17.6 0.8 convolution_convert_fusion.2
  18.4 0.8 convolution_convert_fusion
  20.4 2.0 %collective-permute-start.8 = (bf16[1,1,256,256]{3,2,1,0:T(8,128)(2,1)S(1)}, bf16[1,1,256,256]{3,2,1,0:T(8,128)(2,1)S(1)}, u32[]{:S(2)}, u32[]{:S(2)}) collective-permute-start(bf16[1,1,256,256]{3,2,1,0:T(8,128)(2,1)S(1)} %bitcast.662), channel_id=1, source_target_pairs={{8,0},{12,4},{0,8},{4,12},{9,1},{13,5},{1,9},{5,13},{10,2},{14,6},... | collective-permute-start | bytes 393224 | tf_op jit(solution)/shard_map/ppermute | solution.py:14
  22.6 1.5 %collective-permute-start.7 = (bf16[1,1,256,256]{3,2,1,0:T(8,128)(2,1)S(1)}, bf16[1,1,256,256]{3,2,1,0:T(8,128)(2,1)S(1)}, u32[]{:S(2)}, u32[]{:S(2)}) collective-permute-start(bf16[1,1,256,256]{3,2,1,0:T(8,128)(2,1)S(1)} %bitcast.663), channel_id=1, source_target_pairs={{4,0},{8,4},{12,8},{0,12},{5,1},{9,5},{13,9},{1,13},{6,2},{10,6},{... | collective-permute-start | bytes 393224 | tf_op jit(solution)/shard_map/ppermute | solution.py:14
  24.2 1.5 %collective-permute-start.9 = (bf16[1,1,256,256]{3,2,1,0:T(8,128)(2,1)S(1)}, bf16[1,1,256,256]{3,2,1,0:T(8,128)(2,1)S(1)}, u32[]{:S(2)}, u32[]{:S(2)}) collective-permute-start(bf16[1,1,256,256]{3,2,1,0:T(8,128)(2,1)S(1)} %bitcast.664), channel_id=1, source_target_pairs={{12,0},{0,4},{4,8},{8,12},{13,1},{1,5},{5,9},{9,13},{14,2},{2,6},{... | collective-permute-start | bytes 393224 | tf_op jit(solution)/shard_map/ppermute | solution.py:14
  25.8 4.6 %collective-permute-done.8 = bf16[1,1,256,256]{3,2,1,0:T(8,128)(2,1)S(1)} collective-permute-done((bf16[1,1,256,256]{3,2,1,0:T(8,128)(2,1)S(1)}, bf16[1,1,256,256]{3,2,1,0:T(8,128)(2,1)S(1)}, u32[]{:S(2)}, u32[]{:S(2)}) %collective-permute-start.8) | collective-permute-done | bytes 131104 | tf_op jit(solution)/shard_map/ppermute | solution.py:14
  30.4 1.5 %collective-permute-start.4 = (bf16[1,1,24,256]{3,2,1,0:T(8,128)(2,1)S(1)}, bf16[1,1,24,256]{3,2,1,0:T(8,128)(2,1)S(1)}, u32[]{:S(2)}, u32[]{:S(2)}) collective-permute-start(bf16[1,1,24,256]{3,2,1,0:T(8,128)(2,1)S(1)} %get-tuple-element.20), channel_id=1, source_target_pairs={{0,1},{1,2},{2,3},{3,0},{4,5},{5,6},{6,7},{7,4},{8,9},{9,10},{10,1... | collective-permute-start | bytes 36872 | tf_op jit(solution)/shard_map/ppermute | solution.py:45
  32.4 2.2 %collective-permute-start.6 = (bf16[1,1,24,256]{3,2,1,0:T(8,128)(2,1)S(1)}, bf16[1,1,24,256]{3,2,1,0:T(8,128)(2,1)S(1)}, u32[]{:S(2)}, u32[]{:S(2)}) collective-permute-start(bf16[1,1,24,256]{3,2,1,0:T(8,128)(2,1)S(1)} %get-tuple-element.21), channel_id=1, source_target_pairs={{0,3},{1,0},{2,1},{3,2},{4,7},{5,4},{6,5},{7,6},{8,11},{9,8},{10,9... | collective-permute-start | bytes 36872 | tf_op jit(solution)/shard_map/ppermute | solution.py:45
  34.7 1.2 collective-permute-done.4
  35.9 2.0 %collective-permute-start.12 = (bf16[1,1,256,256]{3,2,1,0:T(8,128)(2,1)S(1)}, bf16[1,1,256,256]{3,2,1,0:T(8,128)(2,1)S(1)}, u32[]{:S(2)}, u32[]{:S(2)}) collective-permute-start(bf16[1,1,256,256]{3,2,1,0:T(8,128)(2,1)S(1)} %bitcast.667), channel_id=1, source_target_pairs={{12,0},{0,4},{4,8},{8,12},{13,1},{1,5},{5,9},{9,13},{14,2},{2,6},{... | collective-permute-start | bytes 393224 | tf_op jit(solution)/shard_map/ppermute | solution.py:14
  38.0 1.3 %collective-permute-start.17 = (bf16[1,1,256,256]{3,2,1,0:T(8,128)(2,1)S(1)}, bf16[1,1,256,256]{3,2,1,0:T(8,128)(2,1)S(1)}, u32[]{:S(2)}, u32[]{:S(2)}) collective-permute-start(bf16[1,1,256,256]{3,2,1,0:T(8,128)(2,1)S(1)} %bitcast.657), channel_id=1, source_target_pairs={{8,0},{12,4},{0,8},{4,12},{9,1},{13,5},{1,9},{5,13},{10,2},{14,6},... | collective-permute-start | bytes 393224 | tf_op jit(solution)/shard_map/ppermute | solution.py:14
  39.7 1.1 collective-permute-done.12
  41.1 1.8 %collective-permute-start.14 = (bf16[1,1,24,256]{3,2,1,0:T(8,128)(2,1)S(1)}, bf16[1,1,24,256]{3,2,1,0:T(8,128)(2,1)S(1)}, u32[]{:S(2)}, u32[]{:S(2)}) collective-permute-start(bf16[1,1,24,256]{3,2,1,0:T(8,128)(2,1)S(1)} %get-tuple-element.19), channel_id=1, source_target_pairs={{0,2},{1,3},{2,0},{3,1},{4,6},{5,7},{6,4},{7,5},{8,10},{9,11},{10,... | collective-permute-start | bytes 36872 | tf_op jit(solution)/shard_map/ppermute | solution.py:45
  42.9 2.1 %collective-permute-start.15 = (bf16[1,1,24,256]{3,2,1,0:T(8,128)(2,1)S(1)}, bf16[1,1,24,256]{3,2,1,0:T(8,128)(2,1)S(1)}, u32[]{:S(2)}, u32[]{:S(2)}) collective-permute-start(bf16[1,1,24,256]{3,2,1,0:T(8,128)(2,1)S(1)} %get-tuple-element.18), channel_id=1, source_target_pairs={{0,3},{1,0},{2,1},{3,2},{4,7},{5,4},{6,5},{7,6},{8,11},{9,8},{10,9... | collective-permute-start | bytes 36872 | tf_op jit(solution)/shard_map/ppermute | solution.py:45
  45.2 1.4 %collective-permute-done.13 = bf16[1,1,24,256]{3,2,1,0:T(8,128)(2,1)S(1)} collective-permute-done((bf16[1,1,24,256]{3,2,1,0:T(8,128)(2,1)S(1)}, bf16[1,1,24,256]{3,2,1,0:T(8,128)(2,1)S(1)}, u32[]{:S(2)}, u32[]{:S(2)}) %collective-permute-start.13) | collective-permute-done | bytes 12320 | tf_op jit(solution)/shard_map/ppermute | solution.py:45
  46.6 2.9 %collective-permute-start.18 = (bf16[1,1,256,256]{3,2,1,0:T(8,128)(2,1)S(1)}, bf16[1,1,256,256]{3,2,1,0:T(8,128)(2,1)S(1)}, u32[]{:S(2)}, u32[]{:S(2)}) collective-permute-start(bf16[1,1,256,256]{3,2,1,0:T(8,128)(2,1)S(1)} %bitcast.658), channel_id=1, source_target_pairs={{12,0},{0,4},{4,8},{8,12},{13,1},{1,5},{5,9},{9,13},{14,2},{2,6},{... | collective-permute-start | bytes 393224 | tf_op jit(solution)/shard_map/ppermute | solution.py:14
  50.4 2.9 %collective-permute-start.28 = (bf16[1,1,256,256]{3,2,1,0:T(8,128)(2,1)S(1)}, bf16[1,1,256,256]{3,2,1,0:T(8,128)(2,1)S(1)}, u32[]{:S(2)}, u32[]{:S(2)}) collective-permute-start(bf16[1,1,256,256]{3,2,1,0:T(8,128)(2,1)S(1)} %bitcast.659), channel_id=1, source_target_pairs={{4,0},{8,4},{12,8},{0,12},{5,1},{9,5},{13,9},{1,13},{6,2},{10,6},{... | collective-permute-start | bytes 393224 | tf_op jit(solution)/shard_map/ppermute | solution.py:14
  53.7 1.7 %collective-permute-start.30 = (bf16[1,1,256,256]{3,2,1,0:T(8,128)(2,1)S(1)}, bf16[1,1,256,256]{3,2,1,0:T(8,128)(2,1)S(1)}, u32[]{:S(2)}, u32[]{:S(2)}) collective-permute-start(bf16[1,1,256,256]{3,2,1,0:T(8,128)(2,1)S(1)} %bitcast.661), channel_id=1, source_target_pairs={{12,0},{0,4},{4,8},{8,12},{13,1},{1,5},{5,9},{9,13},{14,2},{2,6},{... | collective-permute-start | bytes 393224 | tf_op jit(solution)/shard_map/ppermute | solution.py:14
  55.6 1.3 %collective-permute-done.28 = bf16[1,1,256,256]{3,2,1,0:T(8,128)(2,1)S(1)} collective-permute-done((bf16[1,1,256,256]{3,2,1,0:T(8,128)(2,1)S(1)}, bf16[1,1,256,256]{3,2,1,0:T(8,128)(2,1)S(1)}, u32[]{:S(2)}, u32[]{:S(2)}) %collective-permute-start.28) | collective-permute-done | bytes 131104 | tf_op jit(solution)/shard_map/ppermute | solution.py:14
  57.2 1.6 %collective-permute-done.29 = bf16[1,1,256,256]{3,2,1,0:T(8,128)(2,1)S(1)} collective-permute-done((bf16[1,1,256,256]{3,2,1,0:T(8,128)(2,1)S(1)}, bf16[1,1,256,256]{3,2,1,0:T(8,128)(2,1)S(1)}, u32[]{:S(2)}, u32[]{:S(2)}) %collective-permute-start.29) | collective-permute-done | bytes 131104 | tf_op jit(solution)/shard_map/ppermute | solution.py:14
  58.8 2.2 %collective-permute-start.20 = (bf16[1,1,24,256]{3,2,1,0:T(8,128)(2,1)S(1)}, bf16[1,1,24,256]{3,2,1,0:T(8,128)(2,1)S(1)}, u32[]{:S(2)}, u32[]{:S(2)}) collective-permute-start(bf16[1,1,24,256]{3,2,1,0:T(8,128)(2,1)S(1)} %get-tuple-element.16), channel_id=1, source_target_pairs={{0,2},{1,3},{2,0},{3,1},{4,6},{5,7},{6,4},{7,5},{8,10},{9,11},{10,... | collective-permute-start | bytes 36872 | tf_op jit(solution)/shard_map/ppermute | solution.py:45
  61.3 1.1 collective-permute-done.19
  62.4 2.3 %collective-permute-start.24 = (bf16[1,1,256,256]{3,2,1,0:T(8,128)(2,1)S(1)}, bf16[1,1,256,256]{3,2,1,0:T(8,128)(2,1)S(1)}, u32[]{:S(2)}, u32[]{:S(2)}) collective-permute-start(bf16[1,1,256,256]{3,2,1,0:T(8,128)(2,1)S(1)} %bitcast.652), channel_id=1, source_target_pairs={{12,0},{0,4},{4,8},{8,12},{13,1},{1,5},{5,9},{9,13},{14,2},{2,6},{... | collective-permute-start | bytes 393224 | tf_op jit(solution)/shard_map/ppermute | solution.py:14
  65.1 1.5 %collective-permute-start.32 = (bf16[1,1,24,256]{3,2,1,0:T(8,128)(2,1)S(1)}, bf16[1,1,24,256]{3,2,1,0:T(8,128)(2,1)S(1)}, u32[]{:S(2)}, u32[]{:S(2)}) collective-permute-start(bf16[1,1,24,256]{3,2,1,0:T(8,128)(2,1)S(1)} %get-tuple-element.13), channel_id=1, source_target_pairs={{0,2},{1,3},{2,0},{3,1},{4,6},{5,7},{6,4},{7,5},{8,10},{9,11},{10,... | collective-permute-start | bytes 36872 | tf_op jit(solution)/shard_map/ppermute | solution.py:45
  66.6 1.8 %all_gather.8 = bf16[2,1,24,256]{3,2,1,0:T(8,128)(2,1)S(1)} all-gather(bf16[1,1,24,256]{3,2,1,0:T(8,128)(2,1)S(1)} %add_convert_fusion.1), channel_id=1, replica_groups=mesh['gz'=2,'row'=4,'col'=4] {'gz'}, dimensions={0}, use_global_device_ids=true | all-gather | bytes 36864 | tf_op jit(solution)/shard_map/all_gather | solution.py:162
  68.5 2.9 %collective-permute-start.33 = (bf16[1,1,24,256]{3,2,1,0:T(8,128)(2,1)S(1)}, bf16[1,1,24,256]{3,2,1,0:T(8,128)(2,1)S(1)}, u32[]{:S(2)}, u32[]{:S(2)}) collective-permute-start(bf16[1,1,24,256]{3,2,1,0:T(8,128)(2,1)S(1)} %get-tuple-element.12), channel_id=1, source_target_pairs={{0,3},{1,0},{2,1},{3,2},{4,7},{5,4},{6,5},{7,6},{8,11},{9,8},{10,9... | collective-permute-start | bytes 36872 | tf_op jit(solution)/shard_map/ppermute | solution.py:45
  72.1 1.2 collective-permute-start.26
  73.3 2.8 %collective-permute-start.27 = (bf16[1,1,24,256]{3,2,1,0:T(8,128)(2,1)S(1)}, bf16[1,1,24,256]{3,2,1,0:T(8,128)(2,1)S(1)}, u32[]{:S(2)}, u32[]{:S(2)}) collective-permute-start(bf16[1,1,24,256]{3,2,1,0:T(8,128)(2,1)S(1)} %get-tuple-element.9), channel_id=1, source_target_pairs={{0,3},{1,0},{2,1},{3,2},{4,7},{5,4},{6,5},{7,6},{8,11},{9,8},{10,9... | collective-permute-start | bytes 36872 | tf_op jit(solution)/shard_map/ppermute | solution.py:45
  76.2 1.8 %all_gather.9 = bf16[2,1,24,256]{3,2,1,0:T(8,128)(2,1)S(1)} all-gather(bf16[1,1,24,256]{3,2,1,0:T(8,128)(2,1)S(1)} %add_convert_fusion), channel_id=1, replica_groups=mesh['gz'=2,'row'=4,'col'=4] {'gz'}, dimensions={0}, use_global_device_ids=true | all-gather | bytes 36864 | tf_op jit(solution)/shard_map/all_gather | solution.py:162
  78.2 3.6 %collective-permute-start.34 = (bf16[1,1,24,256]{3,2,1,0:T(8,128)(2,1)S(1)}, bf16[1,1,24,256]{3,2,1,0:T(8,128)(2,1)S(1)}, u32[]{:S(2)}, u32[]{:S(2)}) collective-permute-start(bf16[1,1,24,256]{3,2,1,0:T(8,128)(2,1)S(1)} %fusion.153), channel_id=1, source_target_pairs={{1,0},{2,1},{3,2},{0,3},{5,4},{6,5},{7,6},{4,7},{9,8},{10,9},{11,1... | collective-permute-start | bytes 36872 | tf_op jit(solution)/shard_map/ppermute | solution.py:14
  82.4 5.9 %collective-permute-start.50 = (bf16[1,1,24,256]{3,2,1,0:T(8,128)(2,1)S(1)}, bf16[1,1,24,256]{3,2,1,0:T(8,128)(2,1)S(1)}, u32[]{:S(2)}, u32[]{:S(2)}) collective-permute-start(bf16[1,1,24,256]{3,2,1,0:T(8,128)(2,1)S(1)} %fusion.153), channel_id=1, source_target_pairs={{0,0},{4,1},{8,2},{12,3},{1,4},{5,5},{9,6},{13,7},{2,8},{6,9},{10,... | collective-permute-start | bytes 36872 | tf_op jit(solution)/shard_map/ppermute | solution.py:95
  89.2 3.5 %collective-permute-start.49 = (bf16[1,1,24,256]{3,2,1,0:T(8,128)(2,1)S(1)}, bf16[1,1,24,256]{3,2,1,0:T(8,128)(2,1)S(1)}, u32[]{:S(2)}, u32[]{:S(2)}) collective-permute-start(bf16[1,1,24,256]{3,2,1,0:T(8,128)(2,1)S(1)} %bitcast.672), channel_id=1, source_target_pairs={{0,0},{4,1},{8,2},{12,3},{1,4},{5,5},{9,6},{13,7},{2,8},{6,9},{10,... | collective-permute-start | bytes 36872 | tf_op jit(solution)/shard_map/ppermute | solution.py:95
  92.8 2.5 %collective-permute-start.38 = (bf16[1,1,24,256]{3,2,1,0:T(8,128)(2,1)S(1)}, bf16[1,1,24,256]{3,2,1,0:T(8,128)(2,1)S(1)}, u32[]{:S(2)}, u32[]{:S(2)}) collective-permute-start(bf16[1,1,24,256]{3,2,1,0:T(8,128)(2,1)S(1)} %bitcast.674), channel_id=1, source_target_pairs={{2,0},{3,1},{0,2},{1,3},{6,4},{7,5},{4,6},{5,7},{10,8},{11,9},{8,1... | collective-permute-start | bytes 36872 | tf_op jit(solution)/shard_map/ppermute | solution.py:14
  96.5 1.0 collective-permute-done.38
  97.4 3.3 %collective-permute-done.39 = bf16[1,1,24,256]{3,2,1,0:T(8,128)(2,1)S(1)} collective-permute-done((bf16[1,1,24,256]{3,2,1,0:T(8,128)(2,1)S(1)}, bf16[1,1,24,256]{3,2,1,0:T(8,128)(2,1)S(1)}, u32[]{:S(2)}, u32[]{:S(2)}) %collective-permute-start.39) | collective-permute-done | bytes 12320 | tf_op jit(solution)/shard_map/ppermute | solution.py:14
  101.8 1.9 %collective-permute-start.42 = (bf16[1,1,24,256]{3,2,1,0:T(8,128)(2,1)S(1)}, bf16[1,1,24,256]{3,2,1,0:T(8,128)(2,1)S(1)}, u32[]{:S(2)}, u32[]{:S(2)}) collective-permute-start(bf16[1,1,24,256]{3,2,1,0:T(8,128)(2,1)S(1)} %bitcast.670), channel_id=1, source_target_pairs={{3,0},{0,1},{1,2},{2,3},{7,4},{4,5},{5,6},{6,7},{11,8},{8,9},{9,10... | collective-permute-start | bytes 36872 | tf_op jit(solution)/shard_map/ppermute | solution.py:14
  103.8 6.4 %collective-permute-start.48 = (bf16[1,1,24,256]{3,2,1,0:T(8,128)(2,1)S(1)}, bf16[1,1,24,256]{3,2,1,0:T(8,128)(2,1)S(1)}, u32[]{:S(2)}, u32[]{:S(2)}) collective-permute-start(bf16[1,1,24,256]{3,2,1,0:T(8,128)(2,1)S(1)} %bitcast.671), channel_id=1, source_target_pairs={{0,0},{4,1},{8,2},{12,3},{1,4},{5,5},{9,6},{13,7},{2,8},{6,9},{10,... | collective-permute-start | bytes 36872 | tf_op jit(solution)/shard_map/ppermute | solution.py:95
  111.9 2.0 %collective-permute-start.45 = (bf16[1,1,24,256]{3,2,1,0:T(8,128)(2,1)S(1)}, bf16[1,1,24,256]{3,2,1,0:T(8,128)(2,1)S(1)}, u32[]{:S(2)}, u32[]{:S(2)}) collective-permute-start(bf16[1,1,24,256]{3,2,1,0:T(8,128)(2,1)S(1)} %bitcast.678), channel_id=1, source_target_pairs={{3,0},{0,1},{1,2},{2,3},{7,4},{4,5},{5,6},{6,7},{11,8},{8,9},{9,10... | collective-permute-start | bytes 36872 | tf_op jit(solution)/shard_map/ppermute | solution.py:14
  113.9 4.8 %collective-permute-start.47 = (bf16[1,1,24,256]{3,2,1,0:T(8,128)(2,1)S(1)}, bf16[1,1,24,256]{3,2,1,0:T(8,128)(2,1)S(1)}, u32[]{:S(2)}, u32[]{:S(2)}) collective-permute-start(bf16[1,1,24,256]{3,2,1,0:T(8,128)(2,1)S(1)} %bitcast.679), channel_id=1, source_target_pairs={{0,0},{4,1},{8,2},{12,3},{1,4},{5,5},{9,6},{13,7},{2,8},{6,9},{10,... | collective-permute-start | bytes 36872 | tf_op jit(solution)/shard_map/ppermute | solution.py:95
  120.4 4.6 %collective-permute-start.46 = (bf16[1,1,24,256]{3,2,1,0:T(8,128)(2,1)S(1)}, bf16[1,1,24,256]{3,2,1,0:T(8,128)(2,1)S(1)}, u32[]{:S(2)}, u32[]{:S(2)}) collective-permute-start(bf16[1,1,24,256]{3,2,1,0:T(8,128)(2,1)S(1)} %fusion.158), channel_id=1, source_target_pairs={{0,0},{4,1},{8,2},{12,3},{1,4},{5,5},{9,6},{13,7},{2,8},{6,9},{10,... | collective-permute-start | bytes 36872 | tf_op jit(solution)/shard_map/ppermute | solution.py:95
  125.2 4.4 %collective-permute-done.46 = bf16[1,1,24,256]{3,2,1,0:T(8,128)(2,1)S(1)} collective-permute-done((bf16[1,1,24,256]{3,2,1,0:T(8,128)(2,1)S(1)}, bf16[1,1,24,256]{3,2,1,0:T(8,128)(2,1)S(1)}, u32[]{:S(2)}, u32[]{:S(2)}) %collective-permute-start.46) | collective-permute-done | bytes 12320 | tf_op jit(solution)/shard_map/ppermute | solution.py:95
  (189 shorter events, 16.7 us)
Async XLA Ops:
  3.8 16.6 %collective-permute-start.1 = (bf16[1,1,256,256]{3,2,1,0:T(8,128)(2,1)S(1)}, bf16[1,1,256,256]{3,2,1,0:T(8,128)(2,1)S(1)}, u32[]{:S(2)}, u32[]{:S(2)}) collective-permute-start(bf16[1,1,256,256]{3,2,1,0:T(8,128)(2,1)S(1)} %bitcast.653), channel_id=1, source_target_pairs={{4,0},{8,4},{12,8},{0,12},{5,1},{9,5},{13,9},{1,13},{6,2},{10,6},{... | collective-permute-start | bytes 393224 | tf_op jit(solution)/shard_map/ppermute | solution.py:14
  4.4 18.1 %collective-permute-start.2 = (bf16[1,1,256,256]{3,2,1,0:T(8,128)(2,1)S(1)}, bf16[1,1,256,256]{3,2,1,0:T(8,128)(2,1)S(1)}, u32[]{:S(2)}, u32[]{:S(2)}) collective-permute-start(bf16[1,1,256,256]{3,2,1,0:T(8,128)(2,1)S(1)} %bitcast.654), channel_id=1, source_target_pairs={{8,0},{12,4},{0,8},{4,12},{9,1},{13,5},{1,9},{5,13},{10,2},{14,6},... | collective-permute-start | bytes 393224 | tf_op jit(solution)/shard_map/ppermute | solution.py:14
  4.5 19.7 %collective-permute-start.3 = (bf16[1,1,256,256]{3,2,1,0:T(8,128)(2,1)S(1)}, bf16[1,1,256,256]{3,2,1,0:T(8,128)(2,1)S(1)}, u32[]{:S(2)}, u32[]{:S(2)}) collective-permute-start(bf16[1,1,256,256]{3,2,1,0:T(8,128)(2,1)S(1)} %bitcast.655), channel_id=1, source_target_pairs={{12,0},{0,4},{4,8},{8,12},{13,1},{1,5},{5,9},{9,13},{14,2},{2,6},{... | collective-permute-start | bytes 393224 | tf_op jit(solution)/shard_map/ppermute | solution.py:14
  9.6 10.4 %collective-permute-start = (bf16[5,1,24,256]{3,2,1,0:T(8,128)(2,1)S(1)}, bf16[5,1,24,256]{3,2,1,0:T(8,128)(2,1)S(1)}, u32[]{:S(2)}, u32[]{:S(2)}) collective-permute-start(bf16[5,1,24,256]{3,2,1,0:T(8,128)(2,1)S(1)} %fusion.21), channel_id=1, source_target_pairs={{0,0},{1,4},{2,8},{3,12},{4,1},{5,5},{6,9},{7,13},{8,2},{9,6},{10,... | collective-permute-start | bytes 184328 | tf_op jit(solution)/shard_map/ppermute | solution.py:90
  16.1 23.4 %collective-permute-start.10 = (bf16[1,1,256,256]{3,2,1,0:T(8,128)(2,1)S(1)}, bf16[1,1,256,256]{3,2,1,0:T(8,128)(2,1)S(1)}, u32[]{:S(2)}, u32[]{:S(2)}) collective-permute-start(bf16[1,1,256,256]{3,2,1,0:T(8,128)(2,1)S(1)} %bitcast.665), channel_id=1, source_target_pairs={{4,0},{8,4},{12,8},{0,12},{5,1},{9,5},{13,9},{1,13},{6,2},{10,6},{... | collective-permute-start | bytes 393224 | tf_op jit(solution)/shard_map/ppermute | solution.py:14
  20.0 19.6 %collective-permute-start.11 = (bf16[1,1,256,256]{3,2,1,0:T(8,128)(2,1)S(1)}, bf16[1,1,256,256]{3,2,1,0:T(8,128)(2,1)S(1)}, u32[]{:S(2)}, u32[]{:S(2)}) collective-permute-start(bf16[1,1,256,256]{3,2,1,0:T(8,128)(2,1)S(1)} %bitcast.666), channel_id=1, source_target_pairs={{8,0},{12,4},{0,8},{4,12},{9,1},{13,5},{1,9},{5,13},{10,2},{14,6},... | collective-permute-start | bytes 393224 | tf_op jit(solution)/shard_map/ppermute | solution.py:14
  20.4 10.0 %collective-permute-start.8 = (bf16[1,1,256,256]{3,2,1,0:T(8,128)(2,1)S(1)}, bf16[1,1,256,256]{3,2,1,0:T(8,128)(2,1)S(1)}, u32[]{:S(2)}, u32[]{:S(2)}) collective-permute-start(bf16[1,1,256,256]{3,2,1,0:T(8,128)(2,1)S(1)} %bitcast.662), channel_id=1, source_target_pairs={{8,0},{12,4},{0,8},{4,12},{9,1},{13,5},{1,9},{5,13},{10,2},{14,6},... | collective-permute-start | bytes 393224 | tf_op jit(solution)/shard_map/ppermute | solution.py:14
  22.6 9.5 %collective-permute-start.7 = (bf16[1,1,256,256]{3,2,1,0:T(8,128)(2,1)S(1)}, bf16[1,1,256,256]{3,2,1,0:T(8,128)(2,1)S(1)}, u32[]{:S(2)}, u32[]{:S(2)}) collective-permute-start(bf16[1,1,256,256]{3,2,1,0:T(8,128)(2,1)S(1)} %bitcast.663), channel_id=1, source_target_pairs={{4,0},{8,4},{12,8},{0,12},{5,1},{9,5},{13,9},{1,13},{6,2},{10,6},{... | collective-permute-start | bytes 393224 | tf_op jit(solution)/shard_map/ppermute | solution.py:14
  24.2 8.2 %collective-permute-start.9 = (bf16[1,1,256,256]{3,2,1,0:T(8,128)(2,1)S(1)}, bf16[1,1,256,256]{3,2,1,0:T(8,128)(2,1)S(1)}, u32[]{:S(2)}, u32[]{:S(2)}) collective-permute-start(bf16[1,1,256,256]{3,2,1,0:T(8,128)(2,1)S(1)} %bitcast.664), channel_id=1, source_target_pairs={{12,0},{0,4},{4,8},{8,12},{13,1},{1,5},{5,9},{9,13},{14,2},{2,6},{... | collective-permute-start | bytes 393224 | tf_op jit(solution)/shard_map/ppermute | solution.py:14
  30.4 5.5 %collective-permute-start.4 = (bf16[1,1,24,256]{3,2,1,0:T(8,128)(2,1)S(1)}, bf16[1,1,24,256]{3,2,1,0:T(8,128)(2,1)S(1)}, u32[]{:S(2)}, u32[]{:S(2)}) collective-permute-start(bf16[1,1,24,256]{3,2,1,0:T(8,128)(2,1)S(1)} %get-tuple-element.20), channel_id=1, source_target_pairs={{0,1},{1,2},{2,3},{3,0},{4,5},{5,6},{6,7},{7,4},{8,9},{9,10},{10,1... | collective-permute-start | bytes 36872 | tf_op jit(solution)/shard_map/ppermute | solution.py:45
  32.0 5.9 %collective-permute-start.5 = (bf16[1,1,24,256]{3,2,1,0:T(8,128)(2,1)S(1)}, bf16[1,1,24,256]{3,2,1,0:T(8,128)(2,1)S(1)}, u32[]{:S(2)}, u32[]{:S(2)}) collective-permute-start(bf16[1,1,24,256]{3,2,1,0:T(8,128)(2,1)S(1)} %get-tuple-element.22), channel_id=1, source_target_pairs={{0,2},{1,3},{2,0},{3,1},{4,6},{5,7},{6,4},{7,5},{8,10},{9,11},{10,... | collective-permute-start | bytes 36872 | tf_op jit(solution)/shard_map/ppermute | solution.py:45
  32.4 5.6 %collective-permute-start.6 = (bf16[1,1,24,256]{3,2,1,0:T(8,128)(2,1)S(1)}, bf16[1,1,24,256]{3,2,1,0:T(8,128)(2,1)S(1)}, u32[]{:S(2)}, u32[]{:S(2)}) collective-permute-start(bf16[1,1,24,256]{3,2,1,0:T(8,128)(2,1)S(1)} %get-tuple-element.21), channel_id=1, source_target_pairs={{0,3},{1,0},{2,1},{3,2},{4,7},{5,4},{6,5},{7,6},{8,11},{9,8},{10,9... | collective-permute-start | bytes 36872 | tf_op jit(solution)/shard_map/ppermute | solution.py:45
  35.9 5.0 %collective-permute-start.12 = (bf16[1,1,256,256]{3,2,1,0:T(8,128)(2,1)S(1)}, bf16[1,1,256,256]{3,2,1,0:T(8,128)(2,1)S(1)}, u32[]{:S(2)}, u32[]{:S(2)}) collective-permute-start(bf16[1,1,256,256]{3,2,1,0:T(8,128)(2,1)S(1)} %bitcast.667), channel_id=1, source_target_pairs={{12,0},{0,4},{4,8},{8,12},{13,1},{1,5},{5,9},{9,13},{14,2},{2,6},{... | collective-permute-start | bytes 393224 | tf_op jit(solution)/shard_map/ppermute | solution.py:14
  37.9 12.5 %collective-permute-start.16 = (bf16[1,1,256,256]{3,2,1,0:T(8,128)(2,1)S(1)}, bf16[1,1,256,256]{3,2,1,0:T(8,128)(2,1)S(1)}, u32[]{:S(2)}, u32[]{:S(2)}) collective-permute-start(bf16[1,1,256,256]{3,2,1,0:T(8,128)(2,1)S(1)} %bitcast.656), channel_id=1, source_target_pairs={{4,0},{8,4},{12,8},{0,12},{5,1},{9,5},{13,9},{1,13},{6,2},{10,6},{... | collective-permute-start | bytes 393224 | tf_op jit(solution)/shard_map/ppermute | solution.py:14
  38.0 15.6 %collective-permute-start.17 = (bf16[1,1,256,256]{3,2,1,0:T(8,128)(2,1)S(1)}, bf16[1,1,256,256]{3,2,1,0:T(8,128)(2,1)S(1)}, u32[]{:S(2)}, u32[]{:S(2)}) collective-permute-start(bf16[1,1,256,256]{3,2,1,0:T(8,128)(2,1)S(1)} %bitcast.657), channel_id=1, source_target_pairs={{8,0},{12,4},{0,8},{4,12},{9,1},{13,5},{1,9},{5,13},{10,2},{14,6},... | collective-permute-start | bytes 393224 | tf_op jit(solution)/shard_map/ppermute | solution.py:14
  41.1 5.5 %collective-permute-start.13 = (bf16[1,1,24,256]{3,2,1,0:T(8,128)(2,1)S(1)}, bf16[1,1,24,256]{3,2,1,0:T(8,128)(2,1)S(1)}, u32[]{:S(2)}, u32[]{:S(2)}) collective-permute-start(bf16[1,1,24,256]{3,2,1,0:T(8,128)(2,1)S(1)} %get-tuple-element.17), channel_id=1, source_target_pairs={{0,1},{1,2},{2,3},{3,0},{4,5},{5,6},{6,7},{7,4},{8,9},{9,10},{10,1... | collective-permute-start | bytes 36872 | tf_op jit(solution)/shard_map/ppermute | solution.py:45
  41.1 8.4 %collective-permute-start.14 = (bf16[1,1,24,256]{3,2,1,0:T(8,128)(2,1)S(1)}, bf16[1,1,24,256]{3,2,1,0:T(8,128)(2,1)S(1)}, u32[]{:S(2)}, u32[]{:S(2)}) collective-permute-start(bf16[1,1,24,256]{3,2,1,0:T(8,128)(2,1)S(1)} %get-tuple-element.19), channel_id=1, source_target_pairs={{0,2},{1,3},{2,0},{3,1},{4,6},{5,7},{6,4},{7,5},{8,10},{9,11},{10,... | collective-permute-start | bytes 36872 | tf_op jit(solution)/shard_map/ppermute | solution.py:45
  42.9 6.7 %collective-permute-start.15 = (bf16[1,1,24,256]{3,2,1,0:T(8,128)(2,1)S(1)}, bf16[1,1,24,256]{3,2,1,0:T(8,128)(2,1)S(1)}, u32[]{:S(2)}, u32[]{:S(2)}) collective-permute-start(bf16[1,1,24,256]{3,2,1,0:T(8,128)(2,1)S(1)} %get-tuple-element.18), channel_id=1, source_target_pairs={{0,3},{1,0},{2,1},{3,2},{4,7},{5,4},{6,5},{7,6},{8,11},{9,8},{10,9... | collective-permute-start | bytes 36872 | tf_op jit(solution)/shard_map/ppermute | solution.py:45
  46.6 7.1 %collective-permute-start.18 = (bf16[1,1,256,256]{3,2,1,0:T(8,128)(2,1)S(1)}, bf16[1,1,256,256]{3,2,1,0:T(8,128)(2,1)S(1)}, u32[]{:S(2)}, u32[]{:S(2)}) collective-permute-start(bf16[1,1,256,256]{3,2,1,0:T(8,128)(2,1)S(1)} %bitcast.658), channel_id=1, source_target_pairs={{12,0},{0,4},{4,8},{8,12},{13,1},{1,5},{5,9},{9,13},{14,2},{2,6},{... | collective-permute-start | bytes 393224 | tf_op jit(solution)/shard_map/ppermute | solution.py:14
  49.6 18.9 %collective-permute-start.22 = (bf16[1,1,256,256]{3,2,1,0:T(8,128)(2,1)S(1)}, bf16[1,1,256,256]{3,2,1,0:T(8,128)(2,1)S(1)}, u32[]{:S(2)}, u32[]{:S(2)}) collective-permute-start(bf16[1,1,256,256]{3,2,1,0:T(8,128)(2,1)S(1)} %bitcast.650), channel_id=1, source_target_pairs={{4,0},{8,4},{12,8},{0,12},{5,1},{9,5},{13,9},{1,13},{6,2},{10,6},{... | collective-permute-start | bytes 393224 | tf_op jit(solution)/shard_map/ppermute | solution.py:14
  49.6 21.9 %collective-permute-start.23 = (bf16[1,1,256,256]{3,2,1,0:T(8,128)(2,1)S(1)}, bf16[1,1,256,256]{3,2,1,0:T(8,128)(2,1)S(1)}, u32[]{:S(2)}, u32[]{:S(2)}) collective-permute-start(bf16[1,1,256,256]{3,2,1,0:T(8,128)(2,1)S(1)} %bitcast.651), channel_id=1, source_target_pairs={{8,0},{12,4},{0,8},{4,12},{9,1},{13,5},{1,9},{5,13},{10,2},{14,6},... | collective-permute-start | bytes 393224 | tf_op jit(solution)/shard_map/ppermute | solution.py:14
  50.4 6.5 %collective-permute-start.28 = (bf16[1,1,256,256]{3,2,1,0:T(8,128)(2,1)S(1)}, bf16[1,1,256,256]{3,2,1,0:T(8,128)(2,1)S(1)}, u32[]{:S(2)}, u32[]{:S(2)}) collective-permute-start(bf16[1,1,256,256]{3,2,1,0:T(8,128)(2,1)S(1)} %bitcast.659), channel_id=1, source_target_pairs={{4,0},{8,4},{12,8},{0,12},{5,1},{9,5},{13,9},{1,13},{6,2},{10,6},{... | collective-permute-start | bytes 393224 | tf_op jit(solution)/shard_map/ppermute | solution.py:14
  53.5 5.3 %collective-permute-start.29 = (bf16[1,1,256,256]{3,2,1,0:T(8,128)(2,1)S(1)}, bf16[1,1,256,256]{3,2,1,0:T(8,128)(2,1)S(1)}, u32[]{:S(2)}, u32[]{:S(2)}) collective-permute-start(bf16[1,1,256,256]{3,2,1,0:T(8,128)(2,1)S(1)} %bitcast.660), channel_id=1, source_target_pairs={{8,0},{12,4},{0,8},{4,12},{9,1},{13,5},{1,9},{5,13},{10,2},{14,6},... | collective-permute-start | bytes 393224 | tf_op jit(solution)/shard_map/ppermute | solution.py:14
  53.7 7.4 %collective-permute-start.30 = (bf16[1,1,256,256]{3,2,1,0:T(8,128)(2,1)S(1)}, bf16[1,1,256,256]{3,2,1,0:T(8,128)(2,1)S(1)}, u32[]{:S(2)}, u32[]{:S(2)}) collective-permute-start(bf16[1,1,256,256]{3,2,1,0:T(8,128)(2,1)S(1)} %bitcast.661), channel_id=1, source_target_pairs={{12,0},{0,4},{4,8},{8,12},{13,1},{1,5},{5,9},{9,13},{14,2},{2,6},{... | collective-permute-start | bytes 393224 | tf_op jit(solution)/shard_map/ppermute | solution.py:14
  56.9 5.5 %collective-permute-start.19 = (bf16[1,1,24,256]{3,2,1,0:T(8,128)(2,1)S(1)}, bf16[1,1,24,256]{3,2,1,0:T(8,128)(2,1)S(1)}, u32[]{:S(2)}, u32[]{:S(2)}) collective-permute-start(bf16[1,1,24,256]{3,2,1,0:T(8,128)(2,1)S(1)} %get-tuple-element.14), channel_id=1, source_target_pairs={{0,1},{1,2},{2,3},{3,0},{4,5},{5,6},{6,7},{7,4},{8,9},{9,10},{10,1... | collective-permute-start | bytes 36872 | tf_op jit(solution)/shard_map/ppermute | solution.py:45
  58.8 6.0 %collective-permute-start.20 = (bf16[1,1,24,256]{3,2,1,0:T(8,128)(2,1)S(1)}, bf16[1,1,24,256]{3,2,1,0:T(8,128)(2,1)S(1)}, u32[]{:S(2)}, u32[]{:S(2)}) collective-permute-start(bf16[1,1,24,256]{3,2,1,0:T(8,128)(2,1)S(1)} %get-tuple-element.16), channel_id=1, source_target_pairs={{0,2},{1,3},{2,0},{3,1},{4,6},{5,7},{6,4},{7,5},{8,10},{9,11},{10,... | collective-permute-start | bytes 36872 | tf_op jit(solution)/shard_map/ppermute | solution.py:45
  62.4 9.4 %collective-permute-start.24 = (bf16[1,1,256,256]{3,2,1,0:T(8,128)(2,1)S(1)}, bf16[1,1,256,256]{3,2,1,0:T(8,128)(2,1)S(1)}, u32[]{:S(2)}, u32[]{:S(2)}) collective-permute-start(bf16[1,1,256,256]{3,2,1,0:T(8,128)(2,1)S(1)} %bitcast.652), channel_id=1, source_target_pairs={{12,0},{0,4},{4,8},{8,12},{13,1},{1,5},{5,9},{9,13},{14,2},{2,6},{... | collective-permute-start | bytes 393224 | tf_op jit(solution)/shard_map/ppermute | solution.py:14
  64.8 8.6 %collective-permute-start.31 = (bf16[1,1,24,256]{3,2,1,0:T(8,128)(2,1)S(1)}, bf16[1,1,24,256]{3,2,1,0:T(8,128)(2,1)S(1)}, u32[]{:S(2)}, u32[]{:S(2)}) collective-permute-start(bf16[1,1,24,256]{3,2,1,0:T(8,128)(2,1)S(1)} %get-tuple-element.11), channel_id=1, source_target_pairs={{0,1},{1,2},{2,3},{3,0},{4,5},{5,6},{6,7},{7,4},{8,9},{9,10},{10,1... | collective-permute-start | bytes 36872 | tf_op jit(solution)/shard_map/ppermute | solution.py:45
  65.1 11.1 %collective-permute-start.32 = (bf16[1,1,24,256]{3,2,1,0:T(8,128)(2,1)S(1)}, bf16[1,1,24,256]{3,2,1,0:T(8,128)(2,1)S(1)}, u32[]{:S(2)}, u32[]{:S(2)}) collective-permute-start(bf16[1,1,24,256]{3,2,1,0:T(8,128)(2,1)S(1)} %get-tuple-element.13), channel_id=1, source_target_pairs={{0,2},{1,3},{2,0},{3,1},{4,6},{5,7},{6,4},{7,5},{8,10},{9,11},{10,... | collective-permute-start | bytes 36872 | tf_op jit(solution)/shard_map/ppermute | solution.py:45
  68.5 7.7 %collective-permute-start.33 = (bf16[1,1,24,256]{3,2,1,0:T(8,128)(2,1)S(1)}, bf16[1,1,24,256]{3,2,1,0:T(8,128)(2,1)S(1)}, u32[]{:S(2)}, u32[]{:S(2)}) collective-permute-start(bf16[1,1,24,256]{3,2,1,0:T(8,128)(2,1)S(1)} %get-tuple-element.12), channel_id=1, source_target_pairs={{0,3},{1,0},{2,1},{3,2},{4,7},{5,4},{6,5},{7,6},{8,11},{9,8},{10,9... | collective-permute-start | bytes 36872 | tf_op jit(solution)/shard_map/ppermute | solution.py:45
  72.0 6.0 %collective-permute-start.25 = (bf16[1,1,24,256]{3,2,1,0:T(8,128)(2,1)S(1)}, bf16[1,1,24,256]{3,2,1,0:T(8,128)(2,1)S(1)}, u32[]{:S(2)}, u32[]{:S(2)}) collective-permute-start(bf16[1,1,24,256]{3,2,1,0:T(8,128)(2,1)S(1)} %get-tuple-element.8), channel_id=1, source_target_pairs={{0,1},{1,2},{2,3},{3,0},{4,5},{5,6},{6,7},{7,4},{8,9},{9,10},{10,1... | collective-permute-start | bytes 36872 | tf_op jit(solution)/shard_map/ppermute | solution.py:45
  72.1 6.0 %collective-permute-start.26 = (bf16[1,1,24,256]{3,2,1,0:T(8,128)(2,1)S(1)}, bf16[1,1,24,256]{3,2,1,0:T(8,128)(2,1)S(1)}, u32[]{:S(2)}, u32[]{:S(2)}) collective-permute-start(bf16[1,1,24,256]{3,2,1,0:T(8,128)(2,1)S(1)} %get-tuple-element.10), channel_id=1, source_target_pairs={{0,2},{1,3},{2,0},{3,1},{4,6},{5,7},{6,4},{7,5},{8,10},{9,11},{10,... | collective-permute-start | bytes 36872 | tf_op jit(solution)/shard_map/ppermute | solution.py:45
  73.3 4.8 %collective-permute-start.27 = (bf16[1,1,24,256]{3,2,1,0:T(8,128)(2,1)S(1)}, bf16[1,1,24,256]{3,2,1,0:T(8,128)(2,1)S(1)}, u32[]{:S(2)}, u32[]{:S(2)}) collective-permute-start(bf16[1,1,24,256]{3,2,1,0:T(8,128)(2,1)S(1)} %get-tuple-element.9), channel_id=1, source_target_pairs={{0,3},{1,0},{2,1},{3,2},{4,7},{5,4},{6,5},{7,6},{8,11},{9,8},{10,9... | collective-permute-start | bytes 36872 | tf_op jit(solution)/shard_map/ppermute | solution.py:45
  78.2 10.2 %collective-permute-start.34 = (bf16[1,1,24,256]{3,2,1,0:T(8,128)(2,1)S(1)}, bf16[1,1,24,256]{3,2,1,0:T(8,128)(2,1)S(1)}, u32[]{:S(2)}, u32[]{:S(2)}) collective-permute-start(bf16[1,1,24,256]{3,2,1,0:T(8,128)(2,1)S(1)} %fusion.153), channel_id=1, source_target_pairs={{1,0},{2,1},{3,2},{0,3},{5,4},{6,5},{7,6},{4,7},{9,8},{10,9},{11,1... | collective-permute-start | bytes 36872 | tf_op jit(solution)/shard_map/ppermute | solution.py:14
  81.7 6.6 %collective-permute-start.35 = (bf16[1,1,24,256]{3,2,1,0:T(8,128)(2,1)S(1)}, bf16[1,1,24,256]{3,2,1,0:T(8,128)(2,1)S(1)}, u32[]{:S(2)}, u32[]{:S(2)}) collective-permute-start(bf16[1,1,24,256]{3,2,1,0:T(8,128)(2,1)S(1)} %fusion.153), channel_id=1, source_target_pairs={{2,0},{3,1},{0,2},{1,3},{6,4},{7,5},{4,6},{5,7},{10,8},{11,9},{8,1... | collective-permute-start | bytes 36872 | tf_op jit(solution)/shard_map/ppermute | solution.py:14
  81.7 6.7 %collective-permute-start.36 = (bf16[1,1,24,256]{3,2,1,0:T(8,128)(2,1)S(1)}, bf16[1,1,24,256]{3,2,1,0:T(8,128)(2,1)S(1)}, u32[]{:S(2)}, u32[]{:S(2)}) collective-permute-start(bf16[1,1,24,256]{3,2,1,0:T(8,128)(2,1)S(1)} %fusion.153), channel_id=1, source_target_pairs={{3,0},{0,1},{1,2},{2,3},{7,4},{4,5},{5,6},{6,7},{11,8},{8,9},{9,10... | collective-permute-start | bytes 36872 | tf_op jit(solution)/shard_map/ppermute | solution.py:14
  82.4 13.4 %collective-permute-start.50 = (bf16[1,1,24,256]{3,2,1,0:T(8,128)(2,1)S(1)}, bf16[1,1,24,256]{3,2,1,0:T(8,128)(2,1)S(1)}, u32[]{:S(2)}, u32[]{:S(2)}) collective-permute-start(bf16[1,1,24,256]{3,2,1,0:T(8,128)(2,1)S(1)} %fusion.153), channel_id=1, source_target_pairs={{0,0},{4,1},{8,2},{12,3},{1,4},{5,5},{9,6},{13,7},{2,8},{6,9},{10,... | collective-permute-start | bytes 36872 | tf_op jit(solution)/shard_map/ppermute | solution.py:95
  89.2 21.0 %collective-permute-start.49 = (bf16[1,1,24,256]{3,2,1,0:T(8,128)(2,1)S(1)}, bf16[1,1,24,256]{3,2,1,0:T(8,128)(2,1)S(1)}, u32[]{:S(2)}, u32[]{:S(2)}) collective-permute-start(bf16[1,1,24,256]{3,2,1,0:T(8,128)(2,1)S(1)} %bitcast.672), channel_id=1, source_target_pairs={{0,0},{4,1},{8,2},{12,3},{1,4},{5,5},{9,6},{13,7},{2,8},{6,9},{10,... | collective-permute-start | bytes 36872 | tf_op jit(solution)/shard_map/ppermute | solution.py:95
  95.3 5.5 %collective-permute-start.39 = (bf16[1,1,24,256]{3,2,1,0:T(8,128)(2,1)S(1)}, bf16[1,1,24,256]{3,2,1,0:T(8,128)(2,1)S(1)}, u32[]{:S(2)}, u32[]{:S(2)}) collective-permute-start(bf16[1,1,24,256]{3,2,1,0:T(8,128)(2,1)S(1)} %bitcast.675), channel_id=1, source_target_pairs={{3,0},{0,1},{1,2},{2,3},{7,4},{4,5},{5,6},{6,7},{11,8},{8,9},{9,10... | collective-permute-start | bytes 36872 | tf_op jit(solution)/shard_map/ppermute | solution.py:14
  101.7 9.3 %collective-permute-start.40 = (bf16[1,1,24,256]{3,2,1,0:T(8,128)(2,1)S(1)}, bf16[1,1,24,256]{3,2,1,0:T(8,128)(2,1)S(1)}, u32[]{:S(2)}, u32[]{:S(2)}) collective-permute-start(bf16[1,1,24,256]{3,2,1,0:T(8,128)(2,1)S(1)} %bitcast.668), channel_id=1, source_target_pairs={{1,0},{2,1},{3,2},{0,3},{5,4},{6,5},{7,6},{4,7},{9,8},{10,9},{11,1... | collective-permute-start | bytes 36872 | tf_op jit(solution)/shard_map/ppermute | solution.py:14
  101.8 9.2 %collective-permute-start.41 = (bf16[1,1,24,256]{3,2,1,0:T(8,128)(2,1)S(1)}, bf16[1,1,24,256]{3,2,1,0:T(8,128)(2,1)S(1)}, u32[]{:S(2)}, u32[]{:S(2)}) collective-permute-start(bf16[1,1,24,256]{3,2,1,0:T(8,128)(2,1)S(1)} %bitcast.669), channel_id=1, source_target_pairs={{2,0},{3,1},{0,2},{1,3},{6,4},{7,5},{4,6},{5,7},{10,8},{11,9},{8,1... | collective-permute-start | bytes 36872 | tf_op jit(solution)/shard_map/ppermute | solution.py:14
  101.8 9.2 %collective-permute-start.42 = (bf16[1,1,24,256]{3,2,1,0:T(8,128)(2,1)S(1)}, bf16[1,1,24,256]{3,2,1,0:T(8,128)(2,1)S(1)}, u32[]{:S(2)}, u32[]{:S(2)}) collective-permute-start(bf16[1,1,24,256]{3,2,1,0:T(8,128)(2,1)S(1)} %bitcast.670), channel_id=1, source_target_pairs={{3,0},{0,1},{1,2},{2,3},{7,4},{4,5},{5,6},{6,7},{11,8},{8,9},{9,10... | collective-permute-start | bytes 36872 | tf_op jit(solution)/shard_map/ppermute | solution.py:14
  103.8 15.4 %collective-permute-start.48 = (bf16[1,1,24,256]{3,2,1,0:T(8,128)(2,1)S(1)}, bf16[1,1,24,256]{3,2,1,0:T(8,128)(2,1)S(1)}, u32[]{:S(2)}, u32[]{:S(2)}) collective-permute-start(bf16[1,1,24,256]{3,2,1,0:T(8,128)(2,1)S(1)} %bitcast.671), channel_id=1, source_target_pairs={{0,0},{4,1},{8,2},{12,3},{1,4},{5,5},{9,6},{13,7},{2,8},{6,9},{10,... | collective-permute-start | bytes 36872 | tf_op jit(solution)/shard_map/ppermute | solution.py:95
  111.8 7.6 %collective-permute-start.43 = (bf16[1,1,24,256]{3,2,1,0:T(8,128)(2,1)S(1)}, bf16[1,1,24,256]{3,2,1,0:T(8,128)(2,1)S(1)}, u32[]{:S(2)}, u32[]{:S(2)}) collective-permute-start(bf16[1,1,24,256]{3,2,1,0:T(8,128)(2,1)S(1)} %bitcast.676), channel_id=1, source_target_pairs={{1,0},{2,1},{3,2},{0,3},{5,4},{6,5},{7,6},{4,7},{9,8},{10,9},{11,1... | collective-permute-start | bytes 36872 | tf_op jit(solution)/shard_map/ppermute | solution.py:14
  111.8 7.6 %collective-permute-start.44 = (bf16[1,1,24,256]{3,2,1,0:T(8,128)(2,1)S(1)}, bf16[1,1,24,256]{3,2,1,0:T(8,128)(2,1)S(1)}, u32[]{:S(2)}, u32[]{:S(2)}) collective-permute-start(bf16[1,1,24,256]{3,2,1,0:T(8,128)(2,1)S(1)} %bitcast.677), channel_id=1, source_target_pairs={{2,0},{3,1},{0,2},{1,3},{6,4},{7,5},{4,6},{5,7},{10,8},{11,9},{8,1... | collective-permute-start | bytes 36872 | tf_op jit(solution)/shard_map/ppermute | solution.py:14
  111.9 7.5 %collective-permute-start.45 = (bf16[1,1,24,256]{3,2,1,0:T(8,128)(2,1)S(1)}, bf16[1,1,24,256]{3,2,1,0:T(8,128)(2,1)S(1)}, u32[]{:S(2)}, u32[]{:S(2)}) collective-permute-start(bf16[1,1,24,256]{3,2,1,0:T(8,128)(2,1)S(1)} %bitcast.678), channel_id=1, source_target_pairs={{3,0},{0,1},{1,2},{2,3},{7,4},{4,5},{5,6},{6,7},{11,8},{8,9},{9,10... | collective-permute-start | bytes 36872 | tf_op jit(solution)/shard_map/ppermute | solution.py:14
  113.9 11.2 %collective-permute-start.47 = (bf16[1,1,24,256]{3,2,1,0:T(8,128)(2,1)S(1)}, bf16[1,1,24,256]{3,2,1,0:T(8,128)(2,1)S(1)}, u32[]{:S(2)}, u32[]{:S(2)}) collective-permute-start(bf16[1,1,24,256]{3,2,1,0:T(8,128)(2,1)S(1)} %bitcast.679), channel_id=1, source_target_pairs={{0,0},{4,1},{8,2},{12,3},{1,4},{5,5},{9,6},{13,7},{2,8},{6,9},{10,... | collective-permute-start | bytes 36872 | tf_op jit(solution)/shard_map/ppermute | solution.py:95
  120.4 9.2 %collective-permute-start.46 = (bf16[1,1,24,256]{3,2,1,0:T(8,128)(2,1)S(1)}, bf16[1,1,24,256]{3,2,1,0:T(8,128)(2,1)S(1)}, u32[]{:S(2)}, u32[]{:S(2)}) collective-permute-start(bf16[1,1,24,256]{3,2,1,0:T(8,128)(2,1)S(1)} %fusion.158), channel_id=1, source_target_pairs={{0,0},{4,1},{8,2},{12,3},{1,4},{5,5},{9,6},{13,7},{2,8},{6,9},{10,... | collective-permute-start | bytes 36872 | tf_op jit(solution)/shard_map/ppermute | solution.py:95
  (10 other events, 34.9 us)

commit v2 on v1

--- a/solution.py
+++ b/solution.py
@@ -106,6 +106,96 @@
 
 def pair_of(later, earlier):
     return later * (later - 1) // 2 + earlier
+
+
+def composite(direct, first, second):
+    rows = lax.axis_size("row")
+    r, j = lax.axis_index("row"), lax.axis_index("col")
+    total = 0.0
+    for p in range(rows):
+        part = lax.dynamic_index_in_dim(second, (r + p - j) % rows, 0, False)
+        total = total + jnp.einsum("kjbd,ikde->ijbe", first[p], part, preferred_element_type=F32)
+    return (direct.astype(F32) - total).astype(BF)
+
+
+def col_gather(block):
+    return jnp.stack([ring_from(block, "col", s) for s in range(lax.axis_size("col"))])
+
+
+def packed_row_gather(blocks):
+    got = row_gather(jnp.stack(blocks))
+    return [[g[m] for g in got] for m in range(len(blocks))]
+
+
+def solve_by_tiers(base, factor, share):
+    x0, r1, r2, r3, r4 = base
+    m10, m21, m20 = factor(1, 0), factor(2, 1), factor(2, 0)
+    k0, k1, top = factor(3, 2), factor(4, 2), factor(4, 3)
+    g10, gk0 = packed_row_gather([m10, k0])
+    g21, gtop = packed_row_gather([m21, top])
+    g20 = row_gather(composite(m20, g10, col_gather(m21)))
+    gk1 = row_gather(composite(k1, gk0, col_gather(top)))
+    parts = jnp.stack(
+        [spread(x0, g10), spread(r1, g21) + spread(x0, g20)], axis=1
+    )
+    moved = to_owners(parts, 2)
+    x1 = r1.astype(F32) - moved[0]
+    x2 = r2.astype(F32) - moved[1]
+    h2 = x2.astype(BF)
+    portion = 1.0 / lax.axis_size("gz")
+    parts = jnp.stack(
+        [spread(h2, gk0), spread(h2, gk1) + portion * spread(r3, gtop)], axis=1
+    )
+    both = lax.all_gather(to_owners(parts, 2).astype(BF), "gz").astype(F32)
+    moved = jnp.sum(both, axis=0)
+    x3 = r3.astype(F32) - moved[0]
+    u4 = (r4.astype(F32) - moved[1]).astype(BF)
+    h1 = x1.astype(BF)
+    rel = from_owners(jnp.stack([u4, x3.astype(BF), h1]))
+    u3 = (x3 - collect(rel, 0, gtop)).astype(BF)
+    u2 = (x2 - collect(rel, 1, gk0) - collect(rel, 0, gk1)).astype(BF)
+    late = from_owners(u2[None])
+    early = from_owner_layout(jnp.stack([u2, u3, u4]), share)
+    u1 = (x1 - collect(late, 0, g21)).astype(BF)
+    u0 = (x0.astype(F32) - collect(rel, 2, g10) - collect(late, 0, g20)).astype(BF)
+    last = from_owner_layout(jnp.stack([u0, u1]), share)
+    return [last[0], last[1], early[0], early[1], early[2]]
+
+
+def solve_by_level(base, factor, subs, share):
+    levels = len(base)
+    base = [v.astype(F32) for v in base]
+    pairs = [(a, b) for a in range(levels) for b in range(a) if a < subs or b >= subs - 1]
+    gathered = {ab: row_gather(factor(*ab)) for ab in pairs}
+
+    solved = []
+    for a in range(levels):
+        value = base[a]
+        near = [b for b in range(a) if (a, b) in gathered]
+        own = [b for b in near if a < subs or b >= subs]
+        cross = [b for b in near if b not in own]
+        for group, across in ((own, False), (cross, True)):
+            if group:
+                parts = sum(spread(solved[b].astype(BF), gathered[a, b]) for b in group)
+                total = to_owners(parts[:, None], 1)[0]
+                if across:
+                    both = lax.all_gather(total.astype(BF), "gz").astype(F32)
+                    total = jnp.sum(both, axis=0)
+                value = value - total
+        solved.append(value)
+
+    back = [None] * levels
+    arrived = {}
+    for b in reversed(range(levels)):
+        value = solved[b]
+        for a in range(b + 1, levels):
+            if (a, b) in gathered:
+                value = value - collect(arrived[a], 0, gathered[a, b])
+        back[b] = value.astype(BF)
+        if b:
+            arrived[b] = from_owners(back[b][None])
+
+    return [from_owner_layout(back[l][None], share)[0] for l in range(levels)]
 
 
 def per_device(
@@ -144,42 +234,16 @@
         ]
     )
     owned = into_owner_layout(scaled_rhs, col_blocks)
-    base = [owned[l].astype(F32) for l in range(levels)]
-    pairs = [(a, b) for a in range(levels) for b in range(a) if a < subs or b >= subs - 1]
-    gathered = {ab: row_gather(factor(*ab)) for ab in pairs}
-
-    solved = []
-    for a in range(levels):
-        value = base[a]
-        near = [b for b in range(a) if (a, b) in gathered]
-        own = [b for b in near if a < subs or b >= subs]
-        cross = [b for b in near if b not in own]
-        for group, across in ((own, False), (cross, True)):
-            if group:
-                parts = sum(spread(solved[b].astype(BF), gathered[a, b]) for b in group)
-                total = to_owners(parts[:, None], 1)[0]
-                if across:
-                    both = lax.all_gather(total.astype(BF), "gz").astype(F32)
-                    total = jnp.sum(both, axis=0)
-                value = value - total
-        solved.append(value)
-
-    back = [None] * levels
-    arrived = {}
-    for b in reversed(range(levels)):
-        value = solved[b]
-        for a in range(b + 1, levels):
-            if (a, b) in gathered:
-                value = value - collect(arrived[a], 0, gathered[a, b])
-        back[b] = value.astype(BF)
-        if b:
-            arrived[b] = from_owners(back[b][None])
+    base = [owned[l] for l in range(levels)]
+    if subs == 3 and tops == 2 and lax.axis_size("row") == lax.axis_size("col"):
+        native = solve_by_tiers(base, factor, share)
+    else:
+        native = solve_by_level(base, factor, subs, share)
 
     answers = []
     for l in range(levels):
-        rows_back = from_owner_layout(back[l][None], share)[0]
         answers.append(
-            jnp.einsum("ind,ibd->inb", rows_back, inverse[l], preferred_element_type=F32)
+            jnp.einsum("ind,ibd->inb", native[l], inverse[l], preferred_element_type=F32)
         )
     return jnp.stack(answers[:subs])[None], jnp.stack(answers[subs:])
 

time: 131 us -> 117 us (0.89)
  starting transfers between devices: 83.1 us -> 52.6 us
  waiting for transfers between devices: 21.8 us -> 36.1 us
  matrix products: 14.6 us -> 18 us
  blocking collectives: 3.65 us -> 1.84 us
    ppermute x5 -> x2, starting transfers between devices: 25.3 us -> 9.44 us  [from_owner_layout(): lax.ppermute(values, ('row', 'col'), [(b, a) for a, b in owner_pairs(rows...]
    ppermute x30 -> x24, waiting for transfers between devices: 13.5 us -> 28.4 us  [ring_from(): lax.ppermute(values, axis, [((d + step) % size, d) for d in range(size)])]
    ppermute x15 -> x6, starting transfers between devices: 18.9 us -> 9.75 us  [to_owners(): got = lax.ppermute(send, 'col', [(d, (d + s) % cols) for d in range(cols)])]
    ppermute x30 -> x24, starting transfers between devices: 33.4 us -> 26.8 us  [ring_from(): lax.ppermute(values, axis, [((d + step) % size, d) for d in range(size)])]
    all_gather x2 -> x1, blocking collectives: 3.65 us -> 1.84 us  [solve_by_tiers(): both = lax.all_gather(to_owners(parts, 2).astype(BF), 'gz').astype(F32)]
    dot_general x6, matrix products: 5.34 us -> 7.03 us  [scaled(): jnp.einsum('ijbd,ide->ijbe', kept, inverse, preferred_element_type=F32)]
    dot_general x5 -> x13, matrix products: 0.82 us -> 2.39 us  [the longest x8 1.53 us: composite(): jnp.einsum('kjbd,ikde->ijbe', first[p], part, preferred_element_type=F32)]
    ppermute x15 -> x6, waiting for transfers between devices: 3.86 us -> 2.91 us  [to_owners(): got = lax.ppermute(send, 'col', [(d, (d + s) % cols) for d in range(cols)])]
  transfers between devices with their start and end apart: 51 -> 33, of which waited for: 12 -> 14; matrix products, arithmetic and copies ran while one was open for 12% -> 15% of each run, Pallas kernels for 0% -> 0%
where the time goes in v2:
time: 117 us
  starting transfers between devices  52.6 us (45%)
  waiting for transfers between devices  36.1 us (31%)
  matrix products  18 us (15%)
  other arithmetic  3.86 us (3%)
  local copies, waits for them, and re-layouts  2.1 us (2%)
  between operations  2.04 us (2%)
  blocking collectives  1.84 us (2%)
    ppermute x24, waiting for transfers between devices, ring_from(): lax.ppermute(values, axis, [((d + step) % size, d) for d in range(size)])  28.4 us
    ppermute x24, starting transfers between devices, ring_from(): lax.ppermute(values, axis, [((d + step) % size, d) for d in range(size)])  26.8 us
    ppermute x6, starting transfers between devices, to_owners(): got = lax.ppermute(send, 'col', [(d, (d + s) % cols) for d in range(cols)])  9.75 us
    ppermute x2, starting transfers between devices, from_owner_layout(): lax.ppermute(values, ('row', 'col'), [(b, a) for a, b in owner_pairs(rows...  9.44 us
    dot_general x6, matrix products, scaled(): jnp.einsum('ijbd,ide->ijbe', kept, inverse, preferred_element_type=F32)  7.03 us
    ppermute x1, starting transfers between devices, into_owner_layout(): return lax.ppermute(values, ('row', 'col'), owner_pairs(rows, cols))  6.68 us
    dot_general x24, matrix products, collect(): jnp.einsum('knd,kjbd->jnb', rel[p, index], g, preferred_element_type=F32)  4.34 us
    ppermute x2, waiting for transfers between devices, from_owner_layout(): lax.ppermute(values, ('row', 'col'), [(b, a) for a, b in owner_pairs(rows...  4.3 us
  transfers between devices with their start and end apart: 33, of which 14 were waited for; matrix products, arithmetic and copies ran while one was open for 15% of the time, Pallas kernels for 0%

profile of v2, /device:TPU:6, one launch (start us, length us, event | category | flops | bytes accessed | tf_op | source)
XLA Modules:
  0.0 116.5 jit_solution(2883749815365821478)
XLA Ops:
  1.4 1.2 %convolution_convert_fusion.2 = bf16[256,256]{1,0:T(8,128)(2,1)S(1)} fusion(bf16[1,1,1,256,256]{4,3,2,1,0:T(8,128)(2,1)} %param.14, bf16[2,1,256,256]{3,2,1,0:T(8,128)(2,1)} %param.16, bf16[]{:T(256)} %bitcast.46), kind=kOutput, calls=%fused_computation.14 | convolution fusion | flops 33685504 | bytes 393728 | tf_op jit(solution)/shard_map/ijbd,ide->ijbe/dot_general | solution.py:28
  2.6 3.7 %collective-permute-start.16 = (bf16[1,1,256,256]{3,2,1,0:T(8,128)(2,1)S(1)}, bf16[1,1,256,256]{3,2,1,0:T(8,128)(2,1)S(1)}, u32[]{:S(2)}, u32[]{:S(2)}) collective-permute-start(bf16[1,1,256,256]{3,2,1,0:T(8,128)(2,1)S(1)} %bitcast.691), channel_id=1, source_target_pairs={{1,0},{2,1},{3,2},{0,3},{5,4},{6,5},{7,6},{4,7},{9,8},{10,9},{11,1... | collective-permute-start | bytes 393224 | tf_op jit(solution)/shard_map/ppermute | solution.py:14
  6.2 1.0 collective-permute-start.18
  7.2 0.6 fusion.257
  7.8 0.7 fusion.258
  8.5 1.7 %convolution_convert_fusion.4 = bf16[256,256]{1,0:T(8,128)(2,1)S(1)} fusion(bf16[1,2,1,1,256,256]{5,4,3,2,1,0:T(8,128)(2,1)} %param.13, bf16[2,1,256,256]{3,2,1,0:T(8,128)(2,1)S(1)} %copy-done, bf16[]{:T(256)} %bitcast.18), kind=kOutput, calls=%fused_computation.16 | convolution fusion | flops 33685504 | bytes 393728 | tf_op jit(solution)/shard_map/ijbd,ide->ijbe/dot_general | solution.py:28
  10.3 1.7 %convolution_convert_fusion.5 = bf16[256,256]{1,0:T(8,128)(2,1)S(1)} fusion(bf16[1,3,1,1,256,256]{5,4,3,2,1,0:T(8,128)(2,1)} %param.12, bf16[1,3,1,256,256]{4,3,2,1,0:T(8,128)(2,1)S(1)} %copy-done.1, bf16[]{:T(256)} %bitcast.16), kind=kOutput, calls=%fused_computation.17 | convolution fusion | flops 33685504 | bytes 393728 | tf_op jit(solution)/shard_map/ijbd,ide->ijbe/dot_general | solution.py:28
  12.0 0.7 pad_maximum_fusion.2
  12.7 0.5 collective-permute-start.1
  13.7 0.7 copy-done.8
  14.7 6.7 %collective-permute-start = (bf16[5,1,24,256]{3,2,1,0:T(8,128)(2,1)S(1)}, bf16[5,1,24,256]{3,2,1,0:T(8,128)(2,1)S(1)}, u32[]{:S(2)}, u32[]{:S(2)}) collective-permute-start(bf16[5,1,24,256]{3,2,1,0:T(8,128)(2,1)S(1)} %fusion.33), channel_id=1, source_target_pairs={{0,0},{1,4},{2,8},{3,12},{4,1},{5,5},{6,9},{7,13},{8,2},{9,6},{10,... | collective-permute-start | bytes 184328 | tf_op jit(solution)/shard_map/ppermute | solution.py:90
  21.5 0.8 fusion.11
  22.4 0.8 convolution_convert_fusion.3
  23.2 0.8 fusion.9
  25.0 5.2 %collective-permute-start.7 = (bf16[1,1,256,256]{3,2,1,0:T(8,128)(2,1)S(1)}, bf16[1,1,256,256]{3,2,1,0:T(8,128)(2,1)S(1)}, u32[]{:S(2)}, u32[]{:S(2)}) collective-permute-start(bf16[1,1,256,256]{3,2,1,0:T(8,128)(2,1)S(1)} %bitcast.699), channel_id=1, source_target_pairs={{1,0},{2,1},{3,2},{0,3},{5,4},{6,5},{7,6},{4,7},{9,8},{10,9},{11,1... | collective-permute-start | bytes 393224 | tf_op jit(solution)/shard_map/ppermute | solution.py:14
  30.2 0.6 collective-permute-start.9
  31.1 2.4 %collective-permute-done.7 = bf16[1,1,256,256]{3,2,1,0:T(8,128)(2,1)S(1)} collective-permute-done((bf16[1,1,256,256]{3,2,1,0:T(8,128)(2,1)S(1)}, bf16[1,1,256,256]{3,2,1,0:T(8,128)(2,1)S(1)}, u32[]{:S(2)}, u32[]{:S(2)}) %collective-permute-start.7) | collective-permute-done | bytes 131104 | tf_op jit(solution)/shard_map/ppermute | solution.py:14
  33.5 0.9 collective-permute-start.2
  34.4 5.4 %collective-permute-done.8 = bf16[1,1,256,256]{3,2,1,0:T(8,128)(2,1)S(1)} collective-permute-done((bf16[1,1,256,256]{3,2,1,0:T(8,128)(2,1)S(1)}, bf16[1,1,256,256]{3,2,1,0:T(8,128)(2,1)S(1)}, u32[]{:S(2)}, u32[]{:S(2)}) %collective-permute-start.8) | collective-permute-done | bytes 131104 | tf_op jit(solution)/shard_map/ppermute | solution.py:14
  40.7 1.5 %collective-permute-start.4 = (bf16[2,1,1,256,256]{4,3,2,1,0:T(8,128)(2,1)S(1)}, bf16[2,1,1,256,256]{4,3,2,1,0:T(8,128)(2,1)S(1)}, u32[]{:S(2)}, u32[]{:S(2)}) collective-permute-start(bf16[2,1,1,256,256]{4,3,2,1,0:T(8,128)(2,1)S(1)} %pad_maximum_fusion.3), channel_id=1, source_target_pairs={{4,0},{8,4},{12,8},{0,12},{5,1},{9,5},{13,9},{1,13},{6,2},{10,6},{... | collective-permute-start | bytes 786440 | tf_op jit(solution)/shard_map/ppermute | solution.py:14
  42.8 1.7 %collective-permute-start.10 = (bf16[1,1,256,256]{3,2,1,0:T(8,128)(2,1)S(1)}, bf16[1,1,256,256]{3,2,1,0:T(8,128)(2,1)S(1)}, u32[]{:S(2)}, u32[]{:S(2)}) collective-permute-start(bf16[1,1,256,256]{3,2,1,0:T(8,128)(2,1)S(1)} %fusion.7), channel_id=1, source_target_pairs={{4,0},{8,4},{12,8},{0,12},{5,1},{9,5},{13,9},{1,13},{6,2},{10,6},{... | collective-permute-start | bytes 393224 | tf_op jit(solution)/shard_map/ppermute | solution.py:14
  46.0 3.0 %collective-permute-done.6 = bf16[2,1,1,256,256]{4,3,2,1,0:T(8,128)(2,1)S(1)} collective-permute-done((bf16[2,1,1,256,256]{4,3,2,1,0:T(8,128)(2,1)S(1)}, bf16[2,1,1,256,256]{4,3,2,1,0:T(8,128)(2,1)S(1)}, u32[]{:S(2)}, u32[]{:S(2)}) %collective-permute-start.6) | collective-permute-done | bytes 262176 | tf_op jit(solution)/shard_map/ppermute | solution.py:14
  49.0 1.1 collective-permute-start.12
  50.4 8.2 %collective-permute-done.5 = bf16[2,1,1,256,256]{4,3,2,1,0:T(8,128)(2,1)S(1)} collective-permute-done((bf16[2,1,1,256,256]{4,3,2,1,0:T(8,128)(2,1)S(1)}, bf16[2,1,1,256,256]{4,3,2,1,0:T(8,128)(2,1)S(1)}, u32[]{:S(2)}, u32[]{:S(2)}) %collective-permute-start.5) | collective-permute-done | bytes 262176 | tf_op jit(solution)/shard_map/ppermute | solution.py:14
  59.4 1.4 %collective-permute-done.11 = bf16[1,1,256,256]{3,2,1,0:T(8,128)(2,1)S(1)} collective-permute-done((bf16[1,1,256,256]{3,2,1,0:T(8,128)(2,1)S(1)}, bf16[1,1,256,256]{3,2,1,0:T(8,128)(2,1)S(1)}, u32[]{:S(2)}, u32[]{:S(2)}) %collective-permute-start.11) | collective-permute-done | bytes 131104 | tf_op jit(solution)/shard_map/ppermute | solution.py:14
  61.2 3.5 %collective-permute-start.13 = (bf16[2,1,24,256]{3,2,1,0:T(8,128)(2,1)S(1)}, bf16[2,1,24,256]{3,2,1,0:T(8,128)(2,1)S(1)}, u32[]{:S(2)}, u32[]{:S(2)}) collective-permute-start(bf16[2,1,24,256]{3,2,1,0:T(8,128)(2,1)S(1)} %get-tuple-element.13), channel_id=1, source_target_pairs={{0,1},{1,2},{2,3},{3,0},{4,5},{5,6},{6,7},{7,4},{8,9},{9,10},{10,1... | collective-permute-start | bytes 73736 | tf_op jit(solution)/shard_map/ppermute | solution.py:45
  64.7 2.4 %collective-permute-start.15 = (bf16[2,1,24,256]{3,2,1,0:T(8,128)(2,1)S(1)}, bf16[2,1,24,256]{3,2,1,0:T(8,128)(2,1)S(1)}, u32[]{:S(2)}, u32[]{:S(2)}) collective-permute-start(bf16[2,1,24,256]{3,2,1,0:T(8,128)(2,1)S(1)} %get-tuple-element.15), channel_id=1, source_target_pairs={{0,3},{1,0},{2,1},{3,2},{4,7},{5,4},{6,5},{7,6},{8,11},{9,8},{10,9... | collective-permute-start | bytes 73736 | tf_op jit(solution)/shard_map/ppermute | solution.py:45
  67.3 2.7 %collective-permute-start.21 = (bf16[1,1,256,256]{3,2,1,0:T(8,128)(2,1)S(1)}, bf16[1,1,256,256]{3,2,1,0:T(8,128)(2,1)S(1)}, u32[]{:S(2)}, u32[]{:S(2)}) collective-permute-start(bf16[1,1,256,256]{3,2,1,0:T(8,128)(2,1)S(1)} %fusion.6), channel_id=1, source_target_pairs={{12,0},{0,4},{4,8},{8,12},{13,1},{1,5},{5,9},{9,13},{14,2},{2,6},{... | collective-permute-start | bytes 393224 | tf_op jit(solution)/shard_map/ppermute | solution.py:14
  71.2 2.5 %collective-permute-done.21 = bf16[1,1,256,256]{3,2,1,0:T(8,128)(2,1)S(1)} collective-permute-done((bf16[1,1,256,256]{3,2,1,0:T(8,128)(2,1)S(1)}, bf16[1,1,256,256]{3,2,1,0:T(8,128)(2,1)S(1)}, u32[]{:S(2)}, u32[]{:S(2)}) %collective-permute-start.21) | collective-permute-done | bytes 131104 | tf_op jit(solution)/shard_map/ppermute | solution.py:14
  73.9 0.6 fusion.164
  74.5 1.2 %collective-permute-start.22 = (bf16[2,1,24,256]{3,2,0,1:T(8,128)(2,1)}, bf16[2,1,24,256]{3,2,0,1:T(8,128)(2,1)S(1)}, u32[]{:S(2)}, u32[]{:S(2)}) collective-permute-start(bf16[2,1,24,256]{3,2,0,1:T(8,128)(2,1)} %get-tuple-element.10), channel_id=1, source_target_pairs={{0,1},{1,2},{2,3},{3,0},{4,5},{5,6},{6,7},{7,4},{8,9},{9,10},{10,1... | collective-permute-start | bytes 73736 | tf_op jit(solution)/shard_map/ppermute | solution.py:45
  75.7 1.3 %collective-permute-start.23 = (bf16[2,1,24,256]{3,2,0,1:T(8,128)(2,1)}, bf16[2,1,24,256]{3,2,0,1:T(8,128)(2,1)S(1)}, u32[]{:S(2)}, u32[]{:S(2)}) collective-permute-start(bf16[2,1,24,256]{3,2,0,1:T(8,128)(2,1)} %get-tuple-element.11), channel_id=1, source_target_pairs={{0,2},{1,3},{2,0},{3,1},{4,6},{5,7},{6,4},{7,5},{8,10},{9,11},{10,... | collective-permute-start | bytes 73736 | tf_op jit(solution)/shard_map/ppermute | solution.py:45
  77.0 1.3 %collective-permute-start.24 = (bf16[2,1,24,256]{3,2,0,1:T(8,128)(2,1)}, bf16[2,1,24,256]{3,2,0,1:T(8,128)(2,1)}, u32[]{:S(2)}, u32[]{:S(2)}) collective-permute-start(bf16[2,1,24,256]{3,2,0,1:T(8,128)(2,1)} %get-tuple-element.12), channel_id=1, source_target_pairs={{0,3},{1,0},{2,1},{3,2},{4,7},{5,4},{6,5},{7,6},{8,11},{9,8},{10,9... | collective-permute-start | bytes 73736 | tf_op jit(solution)/shard_map/ppermute | solution.py:45
  78.3 2.0 %collective-permute-done.22 = bf16[2,1,24,256]{3,2,0,1:T(8,128)(2,1)S(1)} collective-permute-done((bf16[2,1,24,256]{3,2,0,1:T(8,128)(2,1)}, bf16[2,1,24,256]{3,2,0,1:T(8,128)(2,1)S(1)}, u32[]{:S(2)}, u32[]{:S(2)}) %collective-permute-start.22) | collective-permute-done | bytes 24608 | tf_op jit(solution)/shard_map/ppermute | solution.py:45
  80.3 0.5 collective-permute-done.23
  81.2 0.8 fusion.158
  82.0 1.8 %all-gather = bf16[4,1,24,256]{3,2,1,0:T(8,128)(2,1)S(1)} all-gather(bf16[2,1,24,256]{3,2,1,0:T(8,128)(2,1)S(1)} %fusion.158), channel_id=2, replica_groups=mesh['gz'=2,'row'=4,'col'=4] {'gz'}, dimensions={0}, use_global_device_ids=true | all-gather | bytes 73728 | tf_op jit(solution)/shard_map/all_gather | solution.py:149
  83.9 3.1 %collective-permute-start.25 = (bf16[3,1,24,256]{3,2,0,1:T(8,128)(2,1)S(1)}, bf16[3,1,24,256]{3,2,0,1:T(8,128)(2,1)S(1)}, u32[]{:S(2)}, u32[]{:S(2)}) collective-permute-start(bf16[3,1,24,256]{3,2,0,1:T(8,128)(2,1)S(1)} %get-tuple-element.17), channel_id=1, source_target_pairs={{1,0},{2,1},{3,2},{0,3},{5,4},{6,5},{7,6},{4,7},{9,8},{10,9},{11,1... | collective-permute-start | bytes 110600 | tf_op jit(solution)/shard_map/ppermute | solution.py:14
  87.6 1.2 %collective-permute-done.25 = bf16[3,1,24,256]{3,2,0,1:T(8,128)(2,1)S(1)} collective-permute-done((bf16[3,1,24,256]{3,2,0,1:T(8,128)(2,1)S(1)}, bf16[3,1,24,256]{3,2,0,1:T(8,128)(2,1)S(1)}, u32[]{:S(2)}, u32[]{:S(2)}) %collective-permute-start.25) | collective-permute-done | bytes 36896 | tf_op jit(solution)/shard_map/ppermute | solution.py:14
  88.8 3.2 %collective-permute-done.26 = bf16[3,1,24,256]{3,2,0,1:T(8,128)(2,1)S(1)} collective-permute-done((bf16[3,1,24,256]{3,2,0,1:T(8,128)(2,1)S(1)}, bf16[3,1,24,256]{3,2,0,1:T(8,128)(2,1)S(1)}, u32[]{:S(2)}, u32[]{:S(2)}) %collective-permute-start.26) | collective-permute-done | bytes 36896 | tf_op jit(solution)/shard_map/ppermute | solution.py:14
  92.0 0.9 collective-permute-done.27
  94.5 0.6 collective-permute-start.28
  95.5 2.0 %collective-permute-start.30 = (bf16[1,1,24,256]{3,2,1,0:T(8,128)(2,1)S(1)}, bf16[1,1,24,256]{3,2,1,0:T(8,128)(2,1)S(1)}, u32[]{:S(2)}, u32[]{:S(2)}) collective-permute-start(bf16[1,1,24,256]{3,2,1,0:T(8,128)(2,1)S(1)} %bitcast.712), channel_id=1, source_target_pairs={{3,0},{0,1},{1,2},{2,3},{7,4},{4,5},{5,6},{6,7},{11,8},{8,9},{9,10... | collective-permute-start | bytes 36872 | tf_op jit(solution)/shard_map/ppermute | solution.py:14
  98.2 5.4 %collective-permute-start.32 = (bf16[3,1,24,256]{3,2,1,0:T(8,128)(2,1)S(1)}, bf16[3,1,24,256]{3,2,1,0:T(8,128)(2,1)S(1)}, u32[]{:S(2)}, u32[]{:S(2)}) collective-permute-start(bf16[3,1,24,256]{3,2,1,0:T(8,128)(2,1)S(1)} %pad_maximum_fusion.6), channel_id=1, source_target_pairs={{0,0},{4,1},{8,2},{12,3},{1,4},{5,5},{9,6},{13,7},{2,8},{6,9},{10,... | collective-permute-start | bytes 110600 | tf_op jit(solution)/shard_map/ppermute | solution.py:95
  106.0 4.0 %collective-permute-start.31 = (bf16[2,1,24,256]{3,2,1,0:T(8,128)(2,1)S(1)}, bf16[2,1,24,256]{3,2,1,0:T(8,128)(2,1)S(1)}, u32[]{:S(2)}, u32[]{:S(2)}) collective-permute-start(bf16[2,1,24,256]{3,2,1,0:T(8,128)(2,1)S(1)} %pad_maximum_fusion.7), channel_id=1, source_target_pairs={{0,0},{4,1},{8,2},{12,3},{1,4},{5,5},{9,6},{13,7},{2,8},{6,9},{10,... | collective-permute-start | bytes 73736 | tf_op jit(solution)/shard_map/ppermute | solution.py:95
  110.3 0.7 pad_maximum_fusion.4
  111.0 4.3 %collective-permute-done.31 = bf16[2,1,24,256]{3,2,1,0:T(8,128)(2,1)S(1)} collective-permute-done((bf16[2,1,24,256]{3,2,1,0:T(8,128)(2,1)S(1)}, bf16[2,1,24,256]{3,2,1,0:T(8,128)(2,1)S(1)}, u32[]{:S(2)}, u32[]{:S(2)}) %collective-permute-start.31) | collective-permute-done | bytes 24608 | tf_op jit(solution)/shard_map/ppermute | solution.py:95
  115.8 0.7 maximum_bitcast_fusion
  (156 shorter events, 14.5 us)
Async XLA Ops:
  0.6 7.9 %copy-start = (bf16[2,1,256,256]{3,2,1,0:T(8,128)(2,1)S(1)}, bf16[2,1,256,256]{3,2,1,0:T(8,128)(2,1)}, u32[]{:S(2)}) copy-start(bf16[2,1,256,256]{3,2,1,0:T(8,128)(2,1)} %param.16) | copy-start | bytes 786436
  0.6 6.6 %copy-start.10 = (s32[1,2,1,1]{1,3,2,0:T(1,128)S(1)}, s32[1,2,1,1]{1,3,2,0:T(1,128)}, u32[]{:S(2)}) copy-start(s32[1,2,1,1]{1,3,2,0:T(1,128)} %param.18) | copy-start | bytes 28
  0.7 7.2 %copy-start.11 = (s32[1,3,1,1]{1,3,2,0:T(1,128)S(1)}, s32[1,3,1,1]{1,3,2,0:T(1,128)}, u32[]{:S(2)}) copy-start(s32[1,3,1,1]{1,3,2,0:T(1,128)} %param.17) | copy-start | bytes 40
  1.4 8.9 %copy-start.1 = (bf16[1,3,1,256,256]{4,3,2,1,0:T(8,128)(2,1)S(1)}, bf16[1,3,1,256,256]{4,3,2,1,0:T(8,128)(2,1)}, u32[]{:S(2)}) copy-start(bf16[1,3,1,256,256]{4,3,2,1,0:T(8,128)(2,1)} %param.15) | copy-start | bytes 1179652
  2.6 22.4 %collective-permute-start.16 = (bf16[1,1,256,256]{3,2,1,0:T(8,128)(2,1)S(1)}, bf16[1,1,256,256]{3,2,1,0:T(8,128)(2,1)S(1)}, u32[]{:S(2)}, u32[]{:S(2)}) collective-permute-start(bf16[1,1,256,256]{3,2,1,0:T(8,128)(2,1)S(1)} %bitcast.691), channel_id=1, source_target_pairs={{1,0},{2,1},{3,2},{0,3},{5,4},{6,5},{7,6},{4,7},{9,8},{10,9},{11,1... | collective-permute-start | bytes 393224 | tf_op jit(solution)/shard_map/ppermute | solution.py:14
  6.2 23.9 %collective-permute-start.17 = (bf16[1,1,256,256]{3,2,1,0:T(8,128)(2,1)S(1)}, bf16[1,1,256,256]{3,2,1,0:T(8,128)(2,1)S(1)}, u32[]{:S(2)}, u32[]{:S(2)}) collective-permute-start(bf16[1,1,256,256]{3,2,1,0:T(8,128)(2,1)S(1)} %bitcast.692), channel_id=1, source_target_pairs={{2,0},{3,1},{0,2},{1,3},{6,4},{7,5},{4,6},{5,7},{10,8},{11,9},{8,1... | collective-permute-start | bytes 393224 | tf_op jit(solution)/shard_map/ppermute | solution.py:14
  6.2 23.9 %collective-permute-start.18 = (bf16[1,1,256,256]{3,2,1,0:T(8,128)(2,1)S(1)}, bf16[1,1,256,256]{3,2,1,0:T(8,128)(2,1)S(1)}, u32[]{:S(2)}, u32[]{:S(2)}) collective-permute-start(bf16[1,1,256,256]{3,2,1,0:T(8,128)(2,1)S(1)} %bitcast.693), channel_id=1, source_target_pairs={{3,0},{0,1},{1,2},{2,3},{7,4},{4,5},{5,6},{6,7},{11,8},{8,9},{9,10... | collective-permute-start | bytes 393224 | tf_op jit(solution)/shard_map/ppermute | solution.py:14
  12.0 1.3 %copy-start.6 = (f32[1,3,1,24,256]{4,3,2,1,0:T(8,128)S(1)}, f32[1,3,1,24,256]{4,3,2,1,0:T(8,128)}, u32[]{:S(2)}) copy-start(f32[1,3,1,24,256]{4,3,2,1,0:T(8,128)} %param.10) | copy-start | bytes 221188
  12.7 29.7 %collective-permute-start.1 = (bf16[2,1,1,256,256]{4,3,2,1,0:T(8,128)(2,1)}, bf16[2,1,1,256,256]{4,3,2,1,0:T(8,128)(2,1)S(1)}, u32[]{:S(2)}, u32[]{:S(2)}) collective-permute-start(bf16[2,1,1,256,256]{4,3,2,1,0:T(8,128)(2,1)} %pad_maximum_fusion.2), channel_id=1, source_target_pairs={{4,0},{8,4},{12,8},{0,12},{5,1},{9,5},{13,9},{1,13},{6,2},{10,6},{... | collective-permute-start | bytes 786440 | tf_op jit(solution)/shard_map/ppermute | solution.py:14
  13.5 0.8 copy-start.8
  14.4 7.1 %copy-start.7 = (bf16[1,2,1,1,256,256]{5,4,3,2,1,0:T(8,128)(2,1)S(1)}, bf16[1,2,1,1,256,256]{5,4,3,2,1,0:T(8,128)(2,1)}, u32[]{:S(2)}) copy-start(bf16[1,2,1,1,256,256]{5,4,3,2,1,0:T(8,128)(2,1)} %param.13) | copy-start | bytes 786436
  14.7 7.7 %copy-start.9 = (bf16[1,3,1,1,256,256]{5,4,3,2,1,0:T(8,128)(2,1)S(1)}, bf16[1,3,1,1,256,256]{5,4,3,2,1,0:T(8,128)(2,1)}, u32[]{:S(2)}) copy-start(bf16[1,3,1,1,256,256]{5,4,3,2,1,0:T(8,128)(2,1)} %param.12) | copy-start | bytes 1179652
  14.7 9.9 %collective-permute-start = (bf16[5,1,24,256]{3,2,1,0:T(8,128)(2,1)S(1)}, bf16[5,1,24,256]{3,2,1,0:T(8,128)(2,1)S(1)}, u32[]{:S(2)}, u32[]{:S(2)}) collective-permute-start(bf16[5,1,24,256]{3,2,1,0:T(8,128)(2,1)S(1)} %fusion.33), channel_id=1, source_target_pairs={{0,0},{1,4},{2,8},{3,12},{4,1},{5,5},{6,9},{7,13},{8,2},{9,6},{10,... | collective-permute-start | bytes 184328 | tf_op jit(solution)/shard_map/ppermute | solution.py:90
  24.5 16.2 %collective-permute-start.3 = (bf16[2,1,1,256,256]{4,3,2,1,0:T(8,128)(2,1)}, bf16[2,1,1,256,256]{4,3,2,1,0:T(8,128)(2,1)S(1)}, u32[]{:S(2)}, u32[]{:S(2)}) collective-permute-start(bf16[2,1,1,256,256]{4,3,2,1,0:T(8,128)(2,1)} %pad_maximum_fusion.2), channel_id=1, source_target_pairs={{12,0},{0,4},{4,8},{8,12},{13,1},{1,5},{5,9},{9,13},{14,2},{2,6},{... | collective-permute-start | bytes 786440 | tf_op jit(solution)/shard_map/ppermute | solution.py:14
  25.0 8.6 %collective-permute-start.7 = (bf16[1,1,256,256]{3,2,1,0:T(8,128)(2,1)S(1)}, bf16[1,1,256,256]{3,2,1,0:T(8,128)(2,1)S(1)}, u32[]{:S(2)}, u32[]{:S(2)}) collective-permute-start(bf16[1,1,256,256]{3,2,1,0:T(8,128)(2,1)S(1)} %bitcast.699), channel_id=1, source_target_pairs={{1,0},{2,1},{3,2},{0,3},{5,4},{6,5},{7,6},{4,7},{9,8},{10,9},{11,1... | collective-permute-start | bytes 393224 | tf_op jit(solution)/shard_map/ppermute | solution.py:14
  30.2 9.6 %collective-permute-start.8 = (bf16[1,1,256,256]{3,2,1,0:T(8,128)(2,1)S(1)}, bf16[1,1,256,256]{3,2,1,0:T(8,128)(2,1)S(1)}, u32[]{:S(2)}, u32[]{:S(2)}) collective-permute-start(bf16[1,1,256,256]{3,2,1,0:T(8,128)(2,1)S(1)} %bitcast.700), channel_id=1, source_target_pairs={{2,0},{3,1},{0,2},{1,3},{6,4},{7,5},{4,6},{5,7},{10,8},{11,9},{8,1... | collective-permute-start | bytes 393224 | tf_op jit(solution)/shard_map/ppermute | solution.py:14
  30.2 9.9 %collective-permute-start.9 = (bf16[1,1,256,256]{3,2,1,0:T(8,128)(2,1)S(1)}, bf16[1,1,256,256]{3,2,1,0:T(8,128)(2,1)S(1)}, u32[]{:S(2)}, u32[]{:S(2)}) collective-permute-start(bf16[1,1,256,256]{3,2,1,0:T(8,128)(2,1)S(1)} %bitcast.701), channel_id=1, source_target_pairs={{3,0},{0,1},{1,2},{2,3},{7,4},{4,5},{5,6},{6,7},{11,8},{8,9},{9,10... | collective-permute-start | bytes 393224 | tf_op jit(solution)/shard_map/ppermute | solution.py:14
  33.5 9.1 %collective-permute-start.2 = (bf16[2,1,1,256,256]{4,3,2,1,0:T(8,128)(2,1)}, bf16[2,1,1,256,256]{4,3,2,1,0:T(8,128)(2,1)S(1)}, u32[]{:S(2)}, u32[]{:S(2)}) collective-permute-start(bf16[2,1,1,256,256]{4,3,2,1,0:T(8,128)(2,1)} %pad_maximum_fusion.2), channel_id=1, source_target_pairs={{8,0},{12,4},{0,8},{4,12},{9,1},{13,5},{1,9},{5,13},{10,2},{14,6},... | collective-permute-start | bytes 786440 | tf_op jit(solution)/shard_map/ppermute | solution.py:14
  39.8 9.2 %collective-permute-start.6 = (bf16[2,1,1,256,256]{4,3,2,1,0:T(8,128)(2,1)S(1)}, bf16[2,1,1,256,256]{4,3,2,1,0:T(8,128)(2,1)S(1)}, u32[]{:S(2)}, u32[]{:S(2)}) collective-permute-start(bf16[2,1,1,256,256]{4,3,2,1,0:T(8,128)(2,1)S(1)} %pad_maximum_fusion.3), channel_id=1, source_target_pairs={{12,0},{0,4},{4,8},{8,12},{13,1},{1,5},{5,9},{9,13},{14,2},{2,6},{... | collective-permute-start | bytes 786440 | tf_op jit(solution)/shard_map/ppermute | solution.py:14
  40.0 18.5 %collective-permute-start.5 = (bf16[2,1,1,256,256]{4,3,2,1,0:T(8,128)(2,1)S(1)}, bf16[2,1,1,256,256]{4,3,2,1,0:T(8,128)(2,1)S(1)}, u32[]{:S(2)}, u32[]{:S(2)}) collective-permute-start(bf16[2,1,1,256,256]{4,3,2,1,0:T(8,128)(2,1)S(1)} %pad_maximum_fusion.3), channel_id=1, source_target_pairs={{8,0},{12,4},{0,8},{4,12},{9,1},{13,5},{1,9},{5,13},{10,2},{14,6},... | collective-permute-start | bytes 786440 | tf_op jit(solution)/shard_map/ppermute | solution.py:14
  40.7 18.2 %collective-permute-start.4 = (bf16[2,1,1,256,256]{4,3,2,1,0:T(8,128)(2,1)S(1)}, bf16[2,1,1,256,256]{4,3,2,1,0:T(8,128)(2,1)S(1)}, u32[]{:S(2)}, u32[]{:S(2)}) collective-permute-start(bf16[2,1,1,256,256]{4,3,2,1,0:T(8,128)(2,1)S(1)} %pad_maximum_fusion.3), channel_id=1, source_target_pairs={{4,0},{8,4},{12,8},{0,12},{5,1},{9,5},{13,9},{1,13},{6,2},{10,6},{... | collective-permute-start | bytes 786440 | tf_op jit(solution)/shard_map/ppermute | solution.py:14
  42.8 16.5 %collective-permute-start.10 = (bf16[1,1,256,256]{3,2,1,0:T(8,128)(2,1)S(1)}, bf16[1,1,256,256]{3,2,1,0:T(8,128)(2,1)S(1)}, u32[]{:S(2)}, u32[]{:S(2)}) collective-permute-start(bf16[1,1,256,256]{3,2,1,0:T(8,128)(2,1)S(1)} %fusion.7), channel_id=1, source_target_pairs={{4,0},{8,4},{12,8},{0,12},{5,1},{9,5},{13,9},{1,13},{6,2},{10,6},{... | collective-permute-start | bytes 393224 | tf_op jit(solution)/shard_map/ppermute | solution.py:14
  44.5 16.4 %collective-permute-start.11 = (bf16[1,1,256,256]{3,2,1,0:T(8,128)(2,1)S(1)}, bf16[1,1,256,256]{3,2,1,0:T(8,128)(2,1)S(1)}, u32[]{:S(2)}, u32[]{:S(2)}) collective-permute-start(bf16[1,1,256,256]{3,2,1,0:T(8,128)(2,1)S(1)} %fusion.7), channel_id=1, source_target_pairs={{8,0},{12,4},{0,8},{4,12},{9,1},{13,5},{1,9},{5,13},{10,2},{14,6},... | collective-permute-start | bytes 393224 | tf_op jit(solution)/shard_map/ppermute | solution.py:14
  49.0 12.0 %collective-permute-start.12 = (bf16[1,1,256,256]{3,2,1,0:T(8,128)(2,1)S(1)}, bf16[1,1,256,256]{3,2,1,0:T(8,128)(2,1)S(1)}, u32[]{:S(2)}, u32[]{:S(2)}) collective-permute-start(bf16[1,1,256,256]{3,2,1,0:T(8,128)(2,1)S(1)} %fusion.7), channel_id=1, source_target_pairs={{12,0},{0,4},{4,8},{8,12},{13,1},{1,5},{5,9},{9,13},{14,2},{2,6},{... | collective-permute-start | bytes 393224 | tf_op jit(solution)/shard_map/ppermute | solution.py:14
  58.6 0.7 copy-start.4
  58.6 12.2 %collective-permute-start.19 = (bf16[1,1,256,256]{3,2,1,0:T(8,128)(2,1)S(1)}, bf16[1,1,256,256]{3,2,1,0:T(8,128)(2,1)S(1)}, u32[]{:S(2)}, u32[]{:S(2)}) collective-permute-start(bf16[1,1,256,256]{3,2,1,0:T(8,128)(2,1)S(1)} %fusion.6), channel_id=1, source_target_pairs={{4,0},{8,4},{12,8},{0,12},{5,1},{9,5},{13,9},{1,13},{6,2},{10,6},{... | collective-permute-start | bytes 393224 | tf_op jit(solution)/shard_map/ppermute | solution.py:14
  58.9 8.3 %copy-start.2 = (bf16[2,1,1,256,256]{4,3,2,1,0:T(8,128)(2,1)}, bf16[2,1,1,256,256]{4,3,2,1,0:T(8,128)(2,1)S(1)}, u32[]{:S(2)}) copy-start(bf16[2,1,1,256,256]{4,3,2,1,0:T(8,128)(2,1)S(1)} %collective-permute-done.4) | copy-start | bytes 786436
  58.9 12.1 %collective-permute-start.20 = (bf16[1,1,256,256]{3,2,1,0:T(8,128)(2,1)S(1)}, bf16[1,1,256,256]{3,2,1,0:T(8,128)(2,1)S(1)}, u32[]{:S(2)}, u32[]{:S(2)}) collective-permute-start(bf16[1,1,256,256]{3,2,1,0:T(8,128)(2,1)S(1)} %fusion.6), channel_id=1, source_target_pairs={{8,0},{12,4},{0,8},{4,12},{9,1},{13,5},{1,9},{5,13},{10,2},{14,6},... | collective-permute-start | bytes 393224 | tf_op jit(solution)/shard_map/ppermute | solution.py:14
  61.2 6.1 %collective-permute-start.13 = (bf16[2,1,24,256]{3,2,1,0:T(8,128)(2,1)S(1)}, bf16[2,1,24,256]{3,2,1,0:T(8,128)(2,1)S(1)}, u32[]{:S(2)}, u32[]{:S(2)}) collective-permute-start(bf16[2,1,24,256]{3,2,1,0:T(8,128)(2,1)S(1)} %get-tuple-element.13), channel_id=1, source_target_pairs={{0,1},{1,2},{2,3},{3,0},{4,5},{5,6},{6,7},{7,4},{8,9},{9,10},{10,1... | collective-permute-start | bytes 73736 | tf_op jit(solution)/shard_map/ppermute | solution.py:45
  64.7 5.3 %collective-permute-start.14 = (bf16[2,1,24,256]{3,2,1,0:T(8,128)(2,1)S(1)}, bf16[2,1,24,256]{3,2,1,0:T(8,128)(2,1)S(1)}, u32[]{:S(2)}, u32[]{:S(2)}) collective-permute-start(bf16[2,1,24,256]{3,2,1,0:T(8,128)(2,1)S(1)} %get-tuple-element.14), channel_id=1, source_target_pairs={{0,2},{1,3},{2,0},{3,1},{4,6},{5,7},{6,4},{7,5},{8,10},{9,11},{10,... | collective-permute-start | bytes 73736 | tf_op jit(solution)/shard_map/ppermute | solution.py:45
  64.7 5.3 %collective-permute-start.15 = (bf16[2,1,24,256]{3,2,1,0:T(8,128)(2,1)S(1)}, bf16[2,1,24,256]{3,2,1,0:T(8,128)(2,1)S(1)}, u32[]{:S(2)}, u32[]{:S(2)}) collective-permute-start(bf16[2,1,24,256]{3,2,1,0:T(8,128)(2,1)S(1)} %get-tuple-element.15), channel_id=1, source_target_pairs={{0,3},{1,0},{2,1},{3,2},{4,7},{5,4},{6,5},{7,6},{8,11},{9,8},{10,9... | collective-permute-start | bytes 73736 | tf_op jit(solution)/shard_map/ppermute | solution.py:45
  67.3 6.4 %collective-permute-start.21 = (bf16[1,1,256,256]{3,2,1,0:T(8,128)(2,1)S(1)}, bf16[1,1,256,256]{3,2,1,0:T(8,128)(2,1)S(1)}, u32[]{:S(2)}, u32[]{:S(2)}) collective-permute-start(bf16[1,1,256,256]{3,2,1,0:T(8,128)(2,1)S(1)} %fusion.6), channel_id=1, source_target_pairs={{12,0},{0,4},{4,8},{8,12},{13,1},{1,5},{5,9},{9,13},{14,2},{2,6},{... | collective-permute-start | bytes 393224 | tf_op jit(solution)/shard_map/ppermute | solution.py:14
  74.5 5.8 %collective-permute-start.22 = (bf16[2,1,24,256]{3,2,0,1:T(8,128)(2,1)}, bf16[2,1,24,256]{3,2,0,1:T(8,128)(2,1)S(1)}, u32[]{:S(2)}, u32[]{:S(2)}) collective-permute-start(bf16[2,1,24,256]{3,2,0,1:T(8,128)(2,1)} %get-tuple-element.10), channel_id=1, source_target_pairs={{0,1},{1,2},{2,3},{3,0},{4,5},{5,6},{6,7},{7,4},{8,9},{9,10},{10,1... | collective-permute-start | bytes 73736 | tf_op jit(solution)/shard_map/ppermute | solution.py:45
  75.7 5.1 %collective-permute-start.23 = (bf16[2,1,24,256]{3,2,0,1:T(8,128)(2,1)}, bf16[2,1,24,256]{3,2,0,1:T(8,128)(2,1)S(1)}, u32[]{:S(2)}, u32[]{:S(2)}) collective-permute-start(bf16[2,1,24,256]{3,2,0,1:T(8,128)(2,1)} %get-tuple-element.11), channel_id=1, source_target_pairs={{0,2},{1,3},{2,0},{3,1},{4,6},{5,7},{6,4},{7,5},{8,10},{9,11},{10,... | collective-permute-start | bytes 73736 | tf_op jit(solution)/shard_map/ppermute | solution.py:45
  77.0 4.2 %collective-permute-start.24 = (bf16[2,1,24,256]{3,2,0,1:T(8,128)(2,1)}, bf16[2,1,24,256]{3,2,0,1:T(8,128)(2,1)}, u32[]{:S(2)}, u32[]{:S(2)}) collective-permute-start(bf16[2,1,24,256]{3,2,0,1:T(8,128)(2,1)} %get-tuple-element.12), channel_id=1, source_target_pairs={{0,3},{1,0},{2,1},{3,2},{4,7},{5,4},{6,5},{7,6},{8,11},{9,8},{10,9... | collective-permute-start | bytes 73736 | tf_op jit(solution)/shard_map/ppermute | solution.py:45
  83.9 5.0 %collective-permute-start.25 = (bf16[3,1,24,256]{3,2,0,1:T(8,128)(2,1)S(1)}, bf16[3,1,24,256]{3,2,0,1:T(8,128)(2,1)S(1)}, u32[]{:S(2)}, u32[]{:S(2)}) collective-permute-start(bf16[3,1,24,256]{3,2,0,1:T(8,128)(2,1)S(1)} %get-tuple-element.17), channel_id=1, source_target_pairs={{1,0},{2,1},{3,2},{0,3},{5,4},{6,5},{7,6},{4,7},{9,8},{10,9},{11,1... | collective-permute-start | bytes 110600 | tf_op jit(solution)/shard_map/ppermute | solution.py:14
  87.0 5.1 %collective-permute-start.26 = (bf16[3,1,24,256]{3,2,0,1:T(8,128)(2,1)S(1)}, bf16[3,1,24,256]{3,2,0,1:T(8,128)(2,1)S(1)}, u32[]{:S(2)}, u32[]{:S(2)}) collective-permute-start(bf16[3,1,24,256]{3,2,0,1:T(8,128)(2,1)S(1)} %get-tuple-element.17), channel_id=1, source_target_pairs={{2,0},{3,1},{0,2},{1,3},{6,4},{7,5},{4,6},{5,7},{10,8},{11,9},{8,1... | collective-permute-start | bytes 110600 | tf_op jit(solution)/shard_map/ppermute | solution.py:14
  87.2 5.8 %collective-permute-start.27 = (bf16[3,1,24,256]{3,2,1,0:T(8,128)(2,1)S(1)}, bf16[3,1,24,256]{3,2,1,0:T(8,128)(2,1)S(1)}, u32[]{:S(2)}, u32[]{:S(2)}) collective-permute-start(bf16[3,1,24,256]{3,2,1,0:T(8,128)(2,1)S(1)} %get-tuple-element.16), channel_id=1, source_target_pairs={{3,0},{0,1},{1,2},{2,3},{7,4},{4,5},{5,6},{6,7},{11,8},{8,9},{9,10... | collective-permute-start | bytes 110600 | tf_op jit(solution)/shard_map/ppermute | solution.py:14
  94.1 3.4 %copy-start.3 = (bf16[2,1,1,256,256]{4,3,2,1,0:T(8,128)(2,1)S(1)}, bf16[2,1,1,256,256]{4,3,2,1,0:T(8,128)(2,1)}, u32[]{:S(2)}) copy-start(bf16[2,1,1,256,256]{4,3,2,1,0:T(8,128)(2,1)} %copy-done.2) | copy-start | bytes 786436
  94.5 3.5 %copy-start.5 = (bf16[2,1,1,256,256]{4,3,2,1,0:T(8,128)(2,1)S(1)}, bf16[2,1,1,256,256]{4,3,2,1,0:T(8,128)(2,1)}, u32[]{:S(2)}) copy-start(bf16[2,1,1,256,256]{4,3,2,1,0:T(8,128)(2,1)} %copy-done.4) | copy-start | bytes 786436
  94.5 9.9 %collective-permute-start.28 = (bf16[1,1,24,256]{3,2,1,0:T(8,128)(2,1)S(1)}, bf16[1,1,24,256]{3,2,1,0:T(8,128)(2,1)S(1)}, u32[]{:S(2)}, u32[]{:S(2)}) collective-permute-start(bf16[1,1,24,256]{3,2,1,0:T(8,128)(2,1)S(1)} %bitcast.710), channel_id=1, source_target_pairs={{1,0},{2,1},{3,2},{0,3},{5,4},{6,5},{7,6},{4,7},{9,8},{10,9},{11,1... | collective-permute-start | bytes 36872 | tf_op jit(solution)/shard_map/ppermute | solution.py:14
  95.1 9.3 %collective-permute-start.29 = (bf16[1,1,24,256]{3,2,1,0:T(8,128)(2,1)S(1)}, bf16[1,1,24,256]{3,2,1,0:T(8,128)(2,1)S(1)}, u32[]{:S(2)}, u32[]{:S(2)}) collective-permute-start(bf16[1,1,24,256]{3,2,1,0:T(8,128)(2,1)S(1)} %bitcast.711), channel_id=1, source_target_pairs={{2,0},{3,1},{0,2},{1,3},{6,4},{7,5},{4,6},{5,7},{10,8},{11,9},{8,1... | collective-permute-start | bytes 36872 | tf_op jit(solution)/shard_map/ppermute | solution.py:14
  95.5 8.9 %collective-permute-start.30 = (bf16[1,1,24,256]{3,2,1,0:T(8,128)(2,1)S(1)}, bf16[1,1,24,256]{3,2,1,0:T(8,128)(2,1)S(1)}, u32[]{:S(2)}, u32[]{:S(2)}) collective-permute-start(bf16[1,1,24,256]{3,2,1,0:T(8,128)(2,1)S(1)} %bitcast.712), channel_id=1, source_target_pairs={{3,0},{0,1},{1,2},{2,3},{7,4},{4,5},{5,6},{6,7},{11,8},{8,9},{9,10... | collective-permute-start | bytes 36872 | tf_op jit(solution)/shard_map/ppermute | solution.py:14
  98.2 11.8 %collective-permute-start.32 = (bf16[3,1,24,256]{3,2,1,0:T(8,128)(2,1)S(1)}, bf16[3,1,24,256]{3,2,1,0:T(8,128)(2,1)S(1)}, u32[]{:S(2)}, u32[]{:S(2)}) collective-permute-start(bf16[3,1,24,256]{3,2,1,0:T(8,128)(2,1)S(1)} %pad_maximum_fusion.6), channel_id=1, source_target_pairs={{0,0},{4,1},{8,2},{12,3},{1,4},{5,5},{9,6},{13,7},{2,8},{6,9},{10,... | collective-permute-start | bytes 110600 | tf_op jit(solution)/shard_map/ppermute | solution.py:95
  106.0 9.3 %collective-permute-start.31 = (bf16[2,1,24,256]{3,2,1,0:T(8,128)(2,1)S(1)}, bf16[2,1,24,256]{3,2,1,0:T(8,128)(2,1)S(1)}, u32[]{:S(2)}, u32[]{:S(2)}) collective-permute-start(bf16[2,1,24,256]{3,2,1,0:T(8,128)(2,1)S(1)} %pad_maximum_fusion.7), channel_id=1, source_target_pairs={{0,0},{4,1},{8,2},{12,3},{1,4},{5,5},{9,6},{13,7},{2,8},{6,9},{10,... | collective-permute-start | bytes 73736 | tf_op jit(solution)/shard_map/ppermute | solution.py:95
